TPU v7x, 16 devices: a 4x2x1 block of a 4x4x8 slice. The times are simulated.
16 devices in a mesh: dp: 2 (over y, z), tp: 8 (over x, core).
Axes of the slice: x: 4, y: 2, z: 1, core: 2. Of those that a mesh axis runs over, the one named last changes fastest.
The devices are a block of a 4x4x8 slice.
Arguments:
- hidden: bfloat16 [64, 1536], P('dp'), parts along dimension 0
- lengths: int32 [64], P('dp'), parts along dimension 0
- choice: int32 [2, 64, 8], P(None, 'dp'), parts along dimension 1
- keys_one: bfloat16 [64, 128, 8, 64], P('dp', 'tp'), parts along dimension 0
- vals_one: bfloat16 [64, 128, 8, 64], P('dp', 'tp'), parts along dimension 0
- keys_two: bfloat16 [64, 128, 8, 64], P('dp', 'tp'), parts along dimension 0
- vals_two: bfloat16 [64, 128, 8, 64], P('dp', 'tp'), parts along dimension 0
- g_attn: bfloat16 [2, 1536], replicated
- w_q: bfloat16 [2, 1536, 1536], P(None, None, 'tp')
- w_k: bfloat16 [2, 1536, 512], P(None, None, 'tp')
- w_v: bfloat16 [2, 1536, 512], P(None, None, 'tp')
- w_o: bfloat16 [2, 1536, 1536], P(None, 'tp')
- g_mlp: bfloat16 [2, 1536], replicated
- w_router: bfloat16 [2, 1536, 40], replicated
- w_gate: bfloat16 [2, 40, 1536, 512], P(None, None, None, 'tp')
- w_up: bfloat16 [2, 40, 1536, 512], P(None, None, None, 'tp')
- w_down: bfloat16 [2, 40, 512, 1536], P(None, None, 'tp')
Outputs:
- output 1: bfloat16 [64, 1536], P('dp'), parts along dimension 0
- output 2: bfloat16 [64, 128, 8, 64], P('dp', None, 'tp'), parts along dimension 0
- output 3: bfloat16 [64, 128, 8, 64], P('dp', None, 'tp'), parts along dimension 0
- output 4: bfloat16 [64, 128, 8, 64], P('dp', None, 'tp'), parts along dimension 0
- output 5: bfloat16 [64, 128, 8, 64], P('dp', None, 'tp'), parts along dimension 0
There are 2 independent parts. A program takes and returns all parts, laid end to end along the dimension named above; an argument that names none is the same for every part.
All inputs are finite; a program needn't handle non-finite values.
Results may differ from a plain program's by a relative error of at most 0.02.
Values are sent between devices in bfloat16 or wider.
A program may use at most 768 MiB of HBM per device.

v0:
```python
import jax
import jax.numpy as jnp
from jax import lax
from jax.sharding import PartitionSpec as P

EPS = 1e-5
THETA = 1000000.0


def rms_norm(tensor, gain_vec):
    tensor_f = tensor.astype(jnp.float32)
    scale = lax.rsqrt(jnp.mean(tensor_f * tensor_f, axis=-1, keepdims=True) + EPS)
    return (tensor_f * scale * gain_vec.astype(jnp.float32)).astype(jnp.bfloat16)


def apply_rope(tensor, lengths):
    head_dim = tensor.shape[-1]
    half_dim = head_dim // 2
    inv_freq = THETA ** (-2.0 * jnp.arange(half_dim, dtype=jnp.float32) / head_dim)
    angle = lengths.astype(jnp.float32)[:, None] * inv_freq[None, :]
    cos_part = jnp.cos(angle)[:, None, :]
    sin_part = jnp.sin(angle)[:, None, :]
    lower_half = tensor[..., :half_dim]
    upper_half = tensor[..., half_dim:]
    return jnp.concatenate([lower_half * cos_part - upper_half * sin_part, upper_half * cos_part + lower_half * sin_part], axis=-1)


def expert_block(x_mid, choice, g_mlp, w_router, w_gate, w_up, w_down):
    normed = rms_norm(x_mid, g_mlp)
    logits = jnp.dot(normed, w_router, preferred_element_type=jnp.float32)
    onehot = (choice[:, :, None] == jnp.arange(w_router.shape[1])[None, None, :]).astype(jnp.float32)
    gate_prob = jax.nn.softmax(jnp.sum(onehot * logits[:, None, :], axis=-1), axis=-1)
    gate_mat = jnp.sum(gate_prob[:, :, None] * onehot, axis=1)
    gate_act = jnp.einsum('bd,edf->bef', normed, w_gate, preferred_element_type=jnp.float32)
    up_act = jnp.einsum('bd,edf->bef', normed, w_up, preferred_element_type=jnp.float32)
    expert_in = (jax.nn.silu(gate_act) * up_act * gate_mat[:, :, None]).astype(jnp.bfloat16)
    return jnp.einsum('bef,efd->bd', expert_in, w_down, preferred_element_type=jnp.float32)


def decode_layer(hidden, lengths, choice, key_cache, val_cache, g_attn, w_q, w_k, w_v, w_o, g_mlp, w_router, w_gate, w_up, w_down):
    batch_rows, seq_len, kv_heads, head_dim = key_cache.shape
    num_heads = w_q.shape[1] // head_dim
    normed = rms_norm(hidden, g_attn)
    query_rot = apply_rope(jnp.dot(normed, w_q, preferred_element_type=jnp.float32).reshape(batch_rows, num_heads, head_dim), lengths).astype(jnp.bfloat16)
    key_new = apply_rope(jnp.dot(normed, w_k, preferred_element_type=jnp.float32).reshape(batch_rows, kv_heads, head_dim), lengths).astype(jnp.bfloat16)
    val_new = jnp.dot(normed, w_v, preferred_element_type=jnp.float32).astype(jnp.bfloat16).reshape(batch_rows, kv_heads, head_dim)
    positions = jnp.arange(seq_len)
    is_new = (positions[None, :] == lengths[:, None])[:, :, None, None]
    key_cache = jnp.where(is_new, key_new[:, None], key_cache)
    val_cache = jnp.where(is_new, val_new[:, None], val_cache)
    query_grp = query_rot.reshape(batch_rows, kv_heads, num_heads // kv_heads, head_dim)
    scores = jnp.einsum('bgrd,bsgd->bgrs', query_grp, key_cache, preferred_element_type=jnp.float32) * head_dim ** -0.5
    is_valid = (positions[None, :] <= lengths[:, None])[:, None, None, :]
    attn_prob = jax.nn.softmax(jnp.where(is_valid, scores, -1e30), axis=-1).astype(jnp.bfloat16)
    attn_vec = jnp.einsum('bgrs,bsgd->bgrd', attn_prob, val_cache, preferred_element_type=jnp.float32).astype(jnp.bfloat16).reshape(batch_rows, num_heads * head_dim)
    attn_sum = lax.psum(jnp.dot(attn_vec, w_o, preferred_element_type=jnp.float32).astype(jnp.bfloat16), 'tp')
    x_mid = (hidden.astype(jnp.float32) + attn_sum.astype(jnp.float32)).astype(jnp.bfloat16)
    moe_sum = lax.psum(expert_block(x_mid, choice, g_mlp, w_router, w_gate, w_up, w_down).astype(jnp.bfloat16), 'tp')
    return (x_mid.astype(jnp.float32) + moe_sum.astype(jnp.float32)).astype(jnp.bfloat16), key_cache, val_cache


def solution(mesh):
    seq_spec = P('dp', 'tp', None, None)
    head_spec = P('dp', None, 'tp', None)
    col_spec = P(None, None, 'tp')
    ff_spec = P(None, None, None, 'tp')

    def local_step(hidden, lengths, choice, keys_one, vals_one, keys_two, vals_two, g_attn, w_q, w_k, w_v, w_o, g_mlp, w_router, w_gate, w_up, w_down):
        moved = [lax.all_to_all(cache_blk, 'tp', 2, 1, tiled=True) for cache_blk in (keys_one, vals_one, keys_two, vals_two)]
        results = []
        for layer_idx in range(2):
            hidden, key_cache, val_cache = decode_layer(hidden, lengths, choice[layer_idx], moved[2 * layer_idx], moved[2 * layer_idx + 1], g_attn[layer_idx], w_q[layer_idx], w_k[layer_idx], w_v[layer_idx], w_o[layer_idx], g_mlp[layer_idx], w_router[layer_idx], w_gate[layer_idx], w_up[layer_idx], w_down[layer_idx])
            results.append(key_cache)
            results.append(val_cache)
        return (hidden, results[0], results[1], results[2], results[3])

    return jax.shard_map(local_step, mesh=mesh, in_specs=(P('dp', None), P('dp'), P(None, 'dp', None), seq_spec, seq_spec, seq_spec, seq_spec, P(), col_spec, col_spec, col_spec, P(None, 'tp', None), P(), P(), ff_spec, ff_spec, P(None, None, 'tp', None)), out_specs=(P('dp', None), head_spec, head_spec, head_spec, head_spec), check_vma=False)
```

profile of v0, /device:TPU:113, one launch (start us, length us, event | category | flops | bytes accessed | tf_op | source)
XLA Modules:
  0.0 328.2 jit_solution(825258116050747664)
XLA Ops:
  7.2 1.5 copy.152
  8.7 1.5 reshape.468
  10.2 6.1 %all-to-all-start.1 = ((bf16[8,2,16384]{2,1,0:T(2,128)(2,1)}), bf16[8,2,16384]{2,1,0:T(2,128)(2,1)S(1)}, u32[]{:S(2)}, u32[]{:S(2)}) async-start(bf16[8,2,16384]{2,1,0:T(2,128)(2,1)} %reshape.468), calls=%async_computation.1 | async-start | bytes 1048576 | tf_op jit(solution)/shard_map/all_to_all | solution.py:69
  16.4 1.4 copy.150
  17.7 1.5 reshape.466
  19.4 1.4 copy.153
  20.8 1.5 reshape.470
  22.5 1.1 convolution_bitcast_fusion.1
  23.8 0.9 fusion.157
  24.7 0.4 fusion.118
  25.1 1.4 copy.151
  26.5 1.5 reshape.472
  28.3 0.2 convolution_convert_fusion.5
  28.6 4.8 %all-to-all-start = ((bf16[8,2,16384]{2,1,0:T(2,128)(2,1)}), bf16[8,2,16384]{2,1,0:T(2,128)(2,1)S(1)}, u32[]{:S(2)}, u32[]{:S(2)}) async-start(bf16[8,2,16384]{2,1,0:T(2,128)(2,1)} %reshape.470), calls=%async_computation | async-start | bytes 1048576 | tf_op jit(solution)/shard_map/all_to_all | solution.py:69
  33.5 0.7 reshape.469
  34.1 0.2 bitcast_bitcast_fusion.2
  34.3 8.2 %all-to-all-done = bf16[8,2,16384]{2,1,0:T(2,128)(2,1)S(1)} async-done(((bf16[8,2,16384]{2,1,0:T(2,128)(2,1)}), bf16[8,2,16384]{2,1,0:T(2,128)(2,1)S(1)}, u32[]{:S(2)}, u32[]{:S(2)}) %all-to-all-start) | async-done | bytes 524320 | tf_op jit(solution)/shard_map/all_to_all | solution.py:69
  42.5 5.2 %all-to-all-start.3 = ((bf16[8,2,16384]{2,1,0:T(2,128)(2,1)}), bf16[8,2,16384]{2,1,0:T(2,128)(2,1)}, u32[]{:S(2)}, u32[]{:S(2)}) async-start(bf16[8,2,16384]{2,1,0:T(2,128)(2,1)} %reshape.466), calls=%async_computation.3 | async-start | bytes 1048576 | tf_op jit(solution)/shard_map/all_to_all | solution.py:69
  47.8 0.7 reshape.471
  48.6 0.3 copy.105
  48.9 0.9 fusion.55
  49.8 0.3 copy.109
  50.2 0.2 fusion.158
  50.4 1.1 convolution_convert_fusion.3
  51.6 5.5 %all-to-all-done.3 = bf16[8,2,16384]{2,1,0:T(2,128)(2,1)} async-done(((bf16[8,2,16384]{2,1,0:T(2,128)(2,1)}), bf16[8,2,16384]{2,1,0:T(2,128)(2,1)}, u32[]{:S(2)}, u32[]{:S(2)}) %all-to-all-start.3) | async-done | bytes 524320 | tf_op jit(solution)/shard_map/all_to_all | solution.py:69
  57.1 5.1 %all-to-all-start.2 = ((bf16[8,2,16384]{2,1,0:T(2,128)(2,1)}), bf16[8,2,16384]{2,1,0:T(2,128)(2,1)}, u32[]{:S(2)}, u32[]{:S(2)}) async-start(bf16[8,2,16384]{2,1,0:T(2,128)(2,1)} %reshape.472), calls=%async_computation.2 | async-start | bytes 1048576 | tf_op jit(solution)/shard_map/all_to_all | solution.py:69
  62.2 1.9 convolution_convert_fusion.1
  64.2 0.2 all-reduce.7.cloned.1.call-start
  64.5 2.3 reshape.467
  67.0 4.6 %all-to-all-done.2 = bf16[8,2,16384]{2,1,0:T(2,128)(2,1)} async-done(((bf16[8,2,16384]{2,1,0:T(2,128)(2,1)}), bf16[8,2,16384]{2,1,0:T(2,128)(2,1)}, u32[]{:S(2)}, u32[]{:S(2)}) %all-to-all-start.2) | async-done | bytes 524320 | tf_op jit(solution)/shard_map/all_to_all | solution.py:69
  71.5 2.3 reshape.473
  73.8 42.9 %all-reduce.5.cloned.1.call-done = bf16[32,1536]{1,0:T(8,128)(2,1)} async-done(((bf16[32,1536]{1,0:T(8,128)(2,1)}), bf16[32,1536]{1,0:T(8,128)(2,1)}) %all-reduce.5.cloned.1.call-update) | async-done | bytes 98320 | tf_op jit(solution)/shard_map/psum | solution.py:56
  116.7 1.0 fusion.84
  117.8 1.0 fusion.86
  118.8 7.7 %fusion.12 = f32[32,40,64]{2,0,1:T(8,128)} fusion(bf16[2,40,1536,64]{2,3,1,0:T(8,128)(2,1)} %param.31, bf16[32,1536]{1,0:T(8,128)(2,1)S(1)} %fusion.86), kind=kOutput, calls=%fused_computation.12 | convolution fusion | flops 251658240 | bytes 8290304 | tf_op jit(solution)/shard_map/bd,edf->bef/dot_general | solution.py:34
  126.5 1.0 fusion.106
  127.5 0.2 select_reduce_fusion.3
  128.3 9.3 %fusion.29 = bf16[32,1536]{1,0:T(8,128)(2,1)} fusion(bf16[2,40,64,1536]{3,2,1,0:T(8,128)(2,1)} %param.33, bf16[2,40,1536,64]{2,3,1,0:T(8,128)(2,1)} %param.32, f32[32,40,64]{2,0,1:T(8,128)} %fusion.12, f32[32,40]{0,1:T(8,128)S(1)} %copy.115, bf16[32,1536]{1,0:T(8,128)(2,1)S(1)} %fusion.86), kind=kOutput, calls=%fused_computation.23 | convolution fusion | flops 503939072 | bytes 16585728 | tf_op jit(solution)/shard_map/bef,efd->bd/dot_general | solution.py:37
  137.9 0.3 copy.121
  138.2 0.3 copy.117
  138.5 49.7 %all-reduce.7.cloned.1.call-done = bf16[32,1536]{1,0:T(8,128)(2,1)} async-done(((bf16[32,1536]{1,0:T(8,128)(2,1)}), bf16[32,1536]{1,0:T(8,128)(2,1)}) %all-reduce.7.cloned.1.call-update) | async-done | bytes 98320 | tf_op jit(solution)/shard_map/psum | solution.py:58
  188.2 1.0 fusion.88
  189.3 1.2 convolution_convert_fusion.4
  190.4 1.2 convolution_bitcast_fusion
  191.8 1.4 fusion.113
  193.5 0.9 fusion.54
  194.4 0.2 fusion.159
  194.6 1.1 convolution_convert_fusion.2
  195.8 1.9 convolution_convert_fusion
  197.8 0.3 all-reduce.11.cloned.1.call-start
  198.2 50.3 %all-reduce.9.cloned.1.call-done = bf16[32,1536]{1,0:T(8,128)(2,1)} async-done(((bf16[32,1536]{1,0:T(8,128)(2,1)}), bf16[32,1536]{1,0:T(8,128)(2,1)}) %all-reduce.9.cloned.1.call-update) | async-done | bytes 98320 | tf_op jit(solution)/shard_map/psum | solution.py:56
  248.5 1.0 fusion.92
  249.6 1.0 fusion.94
  250.6 7.7 %fusion.6 = f32[32,40,64]{2,0,1:T(8,128)} fusion(bf16[2,40,1536,64]{2,3,1,0:T(8,128)(2,1)} %param.31, bf16[32,1536]{1,0:T(8,128)(2,1)S(1)} %fusion.94), kind=kOutput, calls=%fused_computation.6 | convolution fusion | flops 251658240 | bytes 8290304 | tf_op jit(solution)/shard_map/bd,edf->bef/dot_general | solution.py:34
  258.3 1.0 fusion.104
  259.3 0.2 select_reduce_fusion.1
  260.1 9.3 %fusion.26 = bf16[32,1536]{1,0:T(8,128)(2,1)} fusion(bf16[2,40,64,1536]{3,2,1,0:T(8,128)(2,1)} %param.33, bf16[2,40,1536,64]{2,3,1,0:T(8,128)(2,1)} %param.32, f32[32,40,64]{2,0,1:T(8,128)} %fusion.6, f32[32,40]{0,1:T(8,128)S(1)} %copy.127, bf16[32,1536]{1,0:T(8,128)(2,1)S(1)} %fusion.94), kind=kOutput, calls=%fused_computation.22 | convolution fusion | flops 503939072 | bytes 16585728 | tf_op jit(solution)/shard_map/bef,efd->bd/dot_general | solution.py:37
  269.5 5.1 %bitcast_select_fusion = (bf16[32,128,1,64]{3,1,0,2:T(8,128)(2,1)}, bf16[32,128,1,64]{3,1,0,2:T(8,128)(2,1)}, bf16[32,128,1,64]{3,1,0,2:T(8,128)(2,1)}, bf16[32,128,1,64]{3,1,0,2:T(8,128)(2,1)}) fusion(bf16[32,8,16,1,64]{4,2,1,0,3:T(8,128)(2,1)S(1)} %copy.121, pred[32,128]{1,0:T(8,128)(4,1)S(1)} %get-tuple-element.50, ...), kind=kLoop, calls=%fused_computation.46 | loop fusion | flops 1048576 | bytes 4214784 | tf_op jit(solution)/shard_map/jit(_where)/select_n | solution.py:50
  274.6 2.3 copy.132
  276.9 2.3 copy.133
  279.3 2.3 copy.134
  281.6 2.3 copy.135
  284.0 36.2 %all-reduce.11.cloned.1.call-done = bf16[32,1536]{1,0:T(8,128)(2,1)} async-done(((bf16[32,1536]{1,0:T(8,128)(2,1)}), bf16[32,1536]{1,0:T(8,128)(2,1)}) %all-reduce.11.cloned.1.call-update) | async-done | bytes 98320 | tf_op jit(solution)/shard_map/psum | solution.py:58
  320.1 1.6 fusion.95
  (72 shorter events, 3.6 us)
Async XLA Ops:
  7.2 12.1 %copy-start.7 = (bf16[2,1536]{1,0:T(2,128)(2,1)S(1)}, bf16[2,1536]{1,0:T(2,128)(2,1)}, u32[]{:S(2)}) copy-start(bf16[2,1536]{1,0:T(2,128)(2,1)} %param.24) | copy-start | bytes 18436
  7.2 12.1 %copy-start.3 = (bf16[32,1536]{1,0:T(8,128)(2,1)S(1)}, bf16[32,1536]{1,0:T(8,128)(2,1)}, u32[]{:S(2)}) copy-start(bf16[32,1536]{1,0:T(8,128)(2,1)} %param.17) | copy-start | bytes 294916
  7.2 15.1 %copy-start.10 = (s32[32]{0:T(128)S(1)}, s32[32]{0:T(128)}, u32[]{:S(2)}) copy-start(s32[32]{0:T(128)} %param.18) | copy-start | bytes 388
  7.2 16.6 %copy-start.4 = (bf16[2,1536,192]{1,2,0:T(8,128)(2,1)S(1)}, bf16[2,1536,192]{1,2,0:T(8,128)(2,1)}, u32[]{:S(2)}) copy-start(bf16[2,1536,192]{1,2,0:T(8,128)(2,1)} %param.25) | copy-start | bytes 3538948
  7.2 17.8 %copy-start.9 = (s32[2,32,8]{1,2,0:T(8,128)S(1)}, s32[2,32,8]{1,2,0:T(8,128)}, u32[]{:S(2)}) copy-start(s32[2,32,8]{1,2,0:T(8,128)} %param.19) | copy-start | bytes 6148
  10.2 18.1 %copy-start.8 = (bf16[2,1536]{1,0:T(2,128)(2,1)S(1)}, bf16[2,1536]{1,0:T(2,128)(2,1)}, u32[]{:S(2)}) copy-start(bf16[2,1536]{1,0:T(2,128)(2,1)} %param.29) | copy-start | bytes 18436
  10.2 18.1 %copy-start.11 = (bf16[2,1536,64]{1,2,0:T(8,128)(2,1)S(1)}, bf16[2,1536,64]{1,2,0:T(8,128)(2,1)}, u32[]{:S(2)}) copy-start(bf16[2,1536,64]{1,2,0:T(8,128)(2,1)} %param.27) | copy-start | bytes 1179652
  10.2 18.4 %all-to-all-start.1 = ((bf16[8,2,16384]{2,1,0:T(2,128)(2,1)}), bf16[8,2,16384]{2,1,0:T(2,128)(2,1)S(1)}, u32[]{:S(2)}, u32[]{:S(2)}) async-start(bf16[8,2,16384]{2,1,0:T(2,128)(2,1)} %reshape.468), calls=%async_computation.1 | async-start | bytes 1048576 | tf_op jit(solution)/shard_map/all_to_all | solution.py:69
  28.6 14.0 %all-to-all-start = ((bf16[8,2,16384]{2,1,0:T(2,128)(2,1)}), bf16[8,2,16384]{2,1,0:T(2,128)(2,1)S(1)}, u32[]{:S(2)}, u32[]{:S(2)}) async-start(bf16[8,2,16384]{2,1,0:T(2,128)(2,1)} %reshape.470), calls=%async_computation | async-start | bytes 1048576 | tf_op jit(solution)/shard_map/all_to_all | solution.py:69
  42.5 14.6 %all-to-all-start.3 = ((bf16[8,2,16384]{2,1,0:T(2,128)(2,1)}), bf16[8,2,16384]{2,1,0:T(2,128)(2,1)}, u32[]{:S(2)}, u32[]{:S(2)}) async-start(bf16[8,2,16384]{2,1,0:T(2,128)(2,1)} %reshape.466), calls=%async_computation.3 | async-start | bytes 1048576 | tf_op jit(solution)/shard_map/all_to_all | solution.py:69
  50.1 14.1 %copy-start = (bf16[32,8,16,1,64]{4,2,1,0,3:T(8,128)(2,1)}, bf16[32,8,16,1,64]{4,2,1,0,3:T(8,128)(2,1)S(1)}, u32[]{:S(2)}) copy-start(bf16[32,8,16,1,64]{4,2,1,0,3:T(8,128)(2,1)S(1)} %copy.109) | copy-start | bytes 1572868
  57.1 14.4 %all-to-all-start.2 = ((bf16[8,2,16384]{2,1,0:T(2,128)(2,1)}), bf16[8,2,16384]{2,1,0:T(2,128)(2,1)}, u32[]{:S(2)}, u32[]{:S(2)}) async-start(bf16[8,2,16384]{2,1,0:T(2,128)(2,1)} %reshape.472), calls=%async_computation.2 | async-start | bytes 1048576 | tf_op jit(solution)/shard_map/all_to_all | solution.py:69
  62.2 54.5 %all-reduce.5.cloned.1.call-start = ((), (), s32[]{:S(2)}) async-start(), calls=%async_computation.4 | async-start | bytes 196608 | tf_op jit(solution)/shard_map/psum | solution.py:56
  64.2 124.0 %all-reduce.7.cloned.1.call-start = ((), (), s32[]{:S(2)}) async-start(), calls=%async_computation.5 | async-start | bytes 196608 | tf_op jit(solution)/shard_map/psum | solution.py:58
  128.3 59.9 %copy-start.6 = (bf16[32,1536]{1,0:T(8,128)(2,1)S(1)}, bf16[32,1536]{1,0:T(8,128)(2,1)}, u32[]{:S(2)}) copy-start(bf16[32,1536]{1,0:T(8,128)(2,1)} %all-reduce.5.cloned.1.call-done) | copy-start | bytes 294916
  137.6 110.9 %all-reduce.9.cloned.1.call-start = ((), (), s32[]{:S(2)}) async-start(), calls=%async_computation.6 | async-start | bytes 196608 | tf_op jit(solution)/shard_map/psum | solution.py:56
  138.5 119.8 %copy-start.2 = (bf16[32,8,16,1,64]{4,2,1,0,3:T(8,128)(2,1)}, bf16[32,8,16,1,64]{4,2,1,0,3:T(8,128)(2,1)S(1)}, u32[]{:S(2)}) copy-start(bf16[32,8,16,1,64]{4,2,1,0,3:T(8,128)(2,1)S(1)} %copy.117) | copy-start | bytes 1572868
  197.8 122.3 %all-reduce.11.cloned.1.call-start = ((), (), s32[]{:S(2)}) async-start(), calls=%async_computation.7 | async-start | bytes 196608 | tf_op jit(solution)/shard_map/psum | solution.py:58
  260.1 9.4 %copy-start.1 = (bf16[32,8,16,1,64]{4,2,1,0,3:T(8,128)(2,1)S(1)}, bf16[32,8,16,1,64]{4,2,1,0,3:T(8,128)(2,1)}, u32[]{:S(2)}) copy-start(bf16[32,8,16,1,64]{4,2,1,0,3:T(8,128)(2,1)} %copy-done) | copy-start | bytes 1572868
  269.4 50.7 %copy-start.5 = (bf16[32,1536]{1,0:T(8,128)(2,1)S(1)}, bf16[32,1536]{1,0:T(8,128)(2,1)}, u32[]{:S(2)}) copy-start(bf16[32,1536]{1,0:T(8,128)(2,1)} %all-reduce.9.cloned.1.call-done) | copy-start | bytes 294916
Sparse Core Ops, SparseCore 0:
  65.9 50.7 all-reduce.4
  137.7 50.4 all-reduce.6
  197.9 50.5 all-reduce.8
  269.6 50.4 all-reduce.10
where the time goes:
time: 331 us; the launch traced here: 328 us
  waiting for transfers between devices  198 us (60%)
  matrix products  49.6 us (15%)
  local copies, waits for them, and re-layouts  30.4 us (9%)
  starting transfers between devices  21.9 us (7%)
  other arithmetic  14.5 us (4%)
  between operations  14.2 us (4%)
    psum x2, waiting for transfers between devices, decode_layer(): lax.psum(jnp.dot(attn_vec, w_o, preferred_element_type=jnp.float32).astyp...  93.2 us
    psum x2, waiting for transfers between devices, decode_layer(): lax.psum(expert_block(x_mid, choice, g_mlp, w_router, w_gate, w_up, w_dow...  85.9 us
    unnamed x40, local copies, waits for them, and re-layouts  26.9 us
    all_to_all x4, starting transfers between devices, local_step(): lax.all_to_all(cache_blk, 'tp', 2, 1, tiled=True)  21.3 us
    dot_general x2, matrix products, expert_block(): jnp.einsum('bef,efd->bd', expert_in, w_down, preferred_element_type=jnp.f...  18.6 us
    all_to_all x4, waiting for transfers between devices, local_step(): lax.all_to_all(cache_blk, 'tp', 2, 1, tiled=True)  18.3 us
    dot_general x2, matrix products, expert_block(): jnp.einsum('bd,edf->bef', normed, w_gate, preferred_element_type=jnp.floa...  15.5 us
  transfers between devices with their start and end apart: 8, of which 7 were waited for; matrix products, arithmetic and copies ran while one was open for 12% of the time, Pallas kernels for 0%

commit v1 on v0

v1 whole, which is shorter than its diff:
```python
import functools

import jax
import jax.numpy as jnp
from jax import lax
from jax.experimental import pallas as pl
from jax.experimental.pallas import tpu as pltpu
from jax.sharding import PartitionSpec as P

EPS = 1e-5
THETA = 1000000.0
MESH = pl.DeviceIdType.MESH
F32 = jnp.float32
BF16 = jnp.bfloat16
CHIPS = 4
OFFSETS = ((2, 0), (2, 1), (1, 0), (3, 0), (1, 1), (3, 1), (0, 1))
CHUNKS = 10


def nt(lhs, rhs):
    return lax.dot_general(lhs, rhs, (((1,), (1,)), ((), ())), preferred_element_type=F32)


def nn(lhs, rhs):
    return jnp.dot(lhs, rhs, preferred_element_type=F32)


def iota(shape, dim):
    return lax.broadcasted_iota(jnp.int32, shape, dim)


def kernel(len_s, hid_h, choice_h, k1_h, v1_h, k2_h, v2_h, ga_h, wq_h, wk_h, wv_h, wo_h, gm_h, wr_h, wg_h, wu_h, wd_h,
           out_hid, ok1, ov1, ok2, ov2,
           hid, choice, ga, gm, xst, sendb, recvb, outst, wqkv, wo, wr, wg, wu, wd,
           qall, kdup, vdup, sc, ov, gexp, ubuf, part, d1, shot, fin,
           sem_small, sem_x, sem_w, sem_wqkv, sem_out, ss_a, rs_a, ss_r, rs_r):
    rows, dim = hid.shape
    half = dim // 2
    seq = recvb.shape[1]
    pos = seq // (2 * CHIPS)
    lanes = recvb.shape[2]
    groups = lanes // 256
    head = 64
    experts = wr.shape[1]
    step = wg.shape[1] // CHUNKS

    me = lax.axis_index("tp")
    chip, core = me // 2, lax.rem(me, 2)
    partner = chip * 2 + 1 - core

    def device(dx, flip):
        return lax.rem(chip + dx, CHIPS) * 2 + (1 - core if flip else core)

    def rcopy(src, dst, ssem, rsem, peer):
        return pltpu.make_async_remote_copy(src, dst, ssem, rsem, device_id={"tp": peer}, device_id_type=MESH)

    barrier = pltpu.get_barrier_semaphore()
    for dx, flip in OFFSETS:
        pl.semaphore_signal(barrier, inc=1, device_id={"tp": device(dx, flip)}, device_id_type=MESH)

    loads = [pltpu.make_async_copy(src, xst.at[c % 3], sem_x.at[c]) for c, src in enumerate((k1_h, v1_h, k2_h, v2_h))]
    small = [pltpu.make_async_copy(src, dst, sem_small.at[n]) for n, (src, dst) in enumerate(
        ((hid_h, hid), (choice_h, choice), (ga_h, ga), (gm_h, gm), (wr_h, wr), (wo_h, wo)))]

    def qkv_loads(layer):
        nq, nk = wq_h.shape[1], wk_h.shape[1]
        return [pltpu.make_async_copy(src.at[layer], wqkv.at[layer, pl.ds(at, size)], sem_wqkv.at[layer, n])
                for n, (src, at, size) in enumerate(((wq_h, 0, nq), (wk_h, nq, nk), (wv_h, nq + nk, nk), (wv_h, nq + 2 * nk, nk)))]

    loads[0].start()
    for copy in small[:4]:
        copy.start()
    for copy in qkv_loads(0):
        copy.start()
    loads[1].start()
    loads[2].start()
    for copy in small[4:]:
        copy.start()
    for copy in qkv_loads(1):
        copy.start()

    def w_copy(layer, which, c):
        src, dst = ((wg_h, wg), (wu_h, wu), (wd_h, wd))[which]
        at = pl.ds(pl.multiple_of(c * step, step), step)
        return pltpu.make_async_copy(src.at[layer, at], dst.at[layer, at], sem_w.at[layer, which, c])

    for layer in range(2):
        def start_weights(c, _, layer=layer):
            w_copy(layer, 0, c).start()
            w_copy(layer, 1, c).start()
            w_copy(layer, 2, c).start()
            return 0
        lax.fori_loop(0, CHUNKS, start_weights, 0)

    def permute(c):
        i, j = iota((128, 128), 0), iota((128, 128), 1)
        perm = (j == lax.rem(i, 16) * 8 + i // 16).astype(BF16)

        def body(t, _):
            tiles = [xst[c % 3, pl.ds(pl.multiple_of(t * 512 + n * 128, 128), 128), :] for n in range(4)]
            moved = nn(perm, jnp.concatenate(tiles, axis=1)).astype(BF16)
            sendb[c, :, :, pl.ds(pl.multiple_of(t * 256, 256), 256)] = moved.reshape(8, pos, 256)
            return 0
        lax.fori_loop(0, groups, body, 0)

    def a2a_copy(c, n):
        peer = device(*OFFSETS[n])
        return rcopy(sendb.at[c, peer], recvb.at[c, pl.ds(pl.multiple_of(me * pos, pos), pos)], ss_a.at[c, n], rs_a.at[c, n], peer)

    def a2a_wait(c):
        for n, (dx, flip) in reversed(list(enumerate(OFFSETS))):
            origin = device(CHIPS - dx, flip)
            rcopy(sendb.at[c, origin], recvb.at[c, pl.ds(pl.multiple_of(origin * pos, pos), pos)], ss_a.at[c, n], rs_a.at[c, n], origin).wait_recv()

    def keep_own(c):
        recvb[c, pl.ds(pl.multiple_of(me * pos, pos), pos), :] = sendb[c, me]

    loads[0].wait()
    permute(0)
    loads[3].start()
    pl.semaphore_wait(barrier, len(OFFSETS))
    for n in range(7):
        a2a_copy(0, n).start()
    loads[1].wait()
    permute(1)
    for n in range(7):
        a2a_copy(1, n).start()
    keep_own(0)
    keep_own(1)

    lane = iota((rows, 128), 1)
    row = iota((rows, 128), 0)
    len_f = jnp.zeros((rows, 128), F32)
    for b in range(rows):
        len_f = jnp.where(row == b, len_s[b].astype(F32), len_f)
    freq = jnp.exp(lax.rem(lane, 32).astype(F32) * (-2.0 / head * 13.815510557964274))
    angle = len_f * freq
    cos_t, sin_t = jnp.cos(angle), jnp.sin(angle)
    low = lax.rem(lane, head) < head // 2
    left = lane < head

    def rope(x):
        turned = jnp.where(low, -pltpu.roll(x, 96, 1), pltpu.roll(x, 32, 1))
        return (x * cos_t + turned * sin_t).astype(BF16).astype(F32)

    def norm(x, gain):
        scale = lax.rsqrt(jnp.mean(x * x, axis=-1, keepdims=True) + EPS)
        return (x * scale * gain.astype(F32)).astype(BF16)

    def project(layer, x):
        for copy in qkv_loads(layer):
            copy.wait()
        qkv = nt(norm(x, ga[layer:layer + 1, :]), wqkv[layer])
        t0, t1 = rope(qkv[:, :128]), rope(qkv[:, 128:256])
        s0, s1 = pltpu.roll(t0, 64, 1), pltpu.roll(t1, 64, 1)
        q3 = jnp.concatenate([jnp.where(left, t0, s0), jnp.where(left, s0, t0), jnp.where(left, t1, s1)], axis=0).astype(BF16)
        kdup[layer] = jnp.where(left, s1, t1)
        vdup[layer] = qkv[:, 256:384].astype(BF16).astype(F32)
        i, j = iota((128, 96), 0), iota((128, 96), 1)
        slot = lax.rem(i, 16)
        pick = (slot < 12) & (j == lax.rem(slot, 3) * rows + i // 16 * 4 + slot // 3)
        dup = nn(pick.astype(BF16), q3)
        slot2, lane2 = lax.rem(iota((128, 256), 0), 16), iota((128, 256), 1)
        both = jnp.concatenate([dup, dup], axis=1)
        qall[layer] = jnp.where(slot2 // 3 == lane2 // 64, both, 0.0).astype(BF16)

    def place_new(c, t, fresh, layer):
        at = pl.ds(pl.multiple_of(t * 256, 256), 256)
        pos_i, lane_i = iota((seq, 128), 0), iota((seq, 128), 1)
        pieces = []
        for n in range(2):
            first = t * 4 + 2 * n
            where_new = jnp.where(lane_i < head, len_s[first], len_s[first + 1])
            line = jnp.where(lane_i[:1] < head, fresh[layer, pl.ds(first, 1), :], fresh[layer, pl.ds(first + 1, 1), :])
            old = recvb[c, :, pl.ds(pl.multiple_of(t * 256 + n * 128, 128), 128)].astype(F32)
            pieces.append(jnp.where(pos_i == where_new, line, old))
        tile = jnp.concatenate(pieces, axis=1).astype(BF16)
        recvb[c, :, at] = tile
        return tile

    def attend(layer):
        ck, cv = 2 * layer, 2 * layer + 1
        a2a_wait(ck)

        def scores(t, _):
            tile = place_new(ck, t, kdup, layer)
            at = pl.ds(pl.multiple_of(t * 16, 16), 16)
            s = nt(qall[layer, at, :], tile) * (head ** -0.5)
            slot, p = iota((16, seq), 0), iota((16, seq), 1)
            limit = jnp.where(slot < 3, len_s[4 * t], jnp.where(slot < 6, len_s[4 * t + 1], jnp.where(slot < 9, len_s[4 * t + 2], len_s[4 * t + 3])))
            sc[at, :] = jnp.where(p <= limit, s, -1e30)
            return 0
        lax.fori_loop(0, groups, scores, 0)
        s = sc[...]
        e = jnp.exp(s - jnp.max(s, axis=-1, keepdims=True))
        sc[...] = e / jnp.sum(e, axis=-1, keepdims=True)
        a2a_wait(cv)

        def values(t, _):
            tile = place_new(cv, t, vdup, layer)
            at = pl.ds(pl.multiple_of(t * 16, 16), 16)
            ov[at, :] = nn(sc[at, :].astype(BF16), tile)
            return 0
        lax.fori_loop(0, groups, values, 0)
        slot2, lane2 = lax.rem(iota((128, 256), 0), 16), iota((128, 256), 1)
        kept = jnp.where(slot2 // 3 == lane2 // 64, ov[...], 0.0)
        both = (kept[:, :128] + kept[:, 128:]).astype(BF16)
        i, j = iota((rows, 128), 0), iota((rows, 128), 1)
        per_head = []
        for r in range(3):
            pick = j == i // 4 * 16 + lax.rem(i, 4) * 3 + r
            got = nn(pick.astype(BF16), both)
            per_head.append(got + pltpu.roll(got, 64, 1))
        return jnp.where(left, per_head[0], per_head[1]).astype(BF16), per_head[2].astype(BF16)[:, :head]

    outs = (ok1, ov1, ok2, ov2)

    def out_copy(c):
        return pltpu.make_async_copy(outst.at[c % 2], outs[c], sem_out.at[c])

    def write_out(c):
        def body(t, _):
            tile = recvb[c, :, pl.ds(pl.multiple_of(t * 256, 256), 256)]
            outst[c % 2, pl.ds(pl.multiple_of(t * 256, 256), 256), :] = tile.T
            return 0
        if c >= 2:
            out_copy(c - 2).wait()
        lax.fori_loop(0, groups, body, 0)
        out_copy(c).start()

    def cols(which):
        return pl.ds(pl.multiple_of(which * half, half), half)

    def all_reduce(r, product, residual, between):
        part[r] = product(1 - core).astype(BF16)
        swap = rcopy(part.at[r], d1.at[r], ss_r.at[r, 0], rs_r.at[r, 0], partner)
        swap.start()
        mine = product(core)
        swap.wait_recv()
        shot[r, chip] = (mine + d1[r].astype(F32)).astype(BF16)
        copies = [swap]
        for n, dx in enumerate((2, 1, 3)):
            copy = rcopy(shot.at[r, chip], shot.at[r, chip], ss_r.at[r, 1 + n], rs_r.at[r, 1 + n], device(dx, 0))
            copy.start()
            copies.append(copy)
        between()
        for n, dx in enumerate((2, 1, 3)):
            origin = lax.rem(chip + CHIPS - dx, CHIPS)
            rcopy(shot.at[r, origin], shot.at[r, origin], ss_r.at[r, 1 + n], rs_r.at[r, 1 + n], device(dx, 0)).wait_recv()
        total = (shot[r, 0].astype(F32) + shot[r, 1].astype(F32)) + (shot[r, 2].astype(F32) + shot[r, 3].astype(F32))
        fin[r, core] = (residual.astype(F32) + total).astype(BF16)
        last = rcopy(fin.at[r, core], fin.at[r, core], ss_r.at[r, 4], rs_r.at[r, 4], partner)
        last.start()
        copies.append(last)
        rcopy(fin.at[r, 1 - core], fin.at[r, 1 - core], ss_r.at[r, 4], rs_r.at[r, 4], partner).wait_recv()
        return copies, jnp.concatenate([fin[r, 0], fin[r, 1]], axis=1).astype(F32)

    def gates(layer, m):
        logits = nt(wr[layer], m)
        e_i = iota((experts, rows), 0)
        chosen = e_i == choice[layer, 0:1, :]
        for n in range(1, choice.shape[1]):
            chosen = chosen | (e_i == choice[layer, n:n + 1, :])
        top = jnp.max(jnp.where(chosen, logits, -3e38), axis=0, keepdims=True)
        weight = jnp.where(chosen, jnp.exp(jnp.where(chosen, logits - top, 0.0)), 0.0)
        gate = (weight / jnp.sum(weight, axis=0, keepdims=True)).T
        for n in range(experts // 2):
            pair = jnp.where(left, gate[:, 2 * n:2 * n + 1], gate[:, 2 * n + 1:2 * n + 2])
            gexp[n // 2, :, (n % 2) * 128:(n % 2 + 1) * 128] = pair

    def experts_up(layer, m):
        def body(c, _):
            w_copy(layer, 0, c).wait()
            w_copy(layer, 1, c).wait()
            at = pl.ds(pl.multiple_of(c * step, step), step)
            g = nt(m, wg[layer, at, :])
            up = nt(m, wu[layer, at, :])
            ubuf[layer, :, at] = (jax.nn.silu(g) * up * gexp[c]).astype(BF16)
            return 0
        lax.fori_loop(0, CHUNKS, body, 0)

        def wait_down(c, _):
            w_copy(layer, 2, c).wait()
            return 0
        lax.fori_loop(0, CHUNKS, wait_down, 0)

    for copy in small:
        copy.wait()
    x = hid[...].astype(F32)
    project(0, x)
    loads[2].wait()
    permute(2)
    loads[3].wait()
    permute(3)
    keep_own(2)
    keep_own(3)

    pending = []
    for layer in range(2):
        if layer:
            project(layer, x)
        first, second = attend(layer)
        n1 = first.shape[1]

        def out_product(which, layer=layer, first=first, second=second, n1=n1):
            return nn(first, wo[layer, :n1, cols(which)]) + nn(second, wo[layer, n1:, cols(which)])

        def between_attn(layer=layer):
            if layer == 0:
                for c in (2, 3):
                    for n in range(7):
                        a2a_copy(c, n).start()
            write_out(2 * layer)
            write_out(2 * layer + 1)

        residual = fin[2 * layer - 1, core] if layer else hid[:, cols(core)]
        copies, x = all_reduce(2 * layer, out_product, residual, between_attn)
        pending += copies
        m = norm(x, gm[layer:layer + 1, :])
        gates(layer, m)
        experts_up(layer, m)

        def down_product(which, layer=layer):
            return nn(ubuf[layer], wd[layer, :, cols(which)])

        copies, x = all_reduce(2 * layer + 1, down_product, fin[2 * layer, core], lambda: None)
        pending += copies
    out_hid[...] = x.astype(BF16)

    for copy in pending:
        copy.wait_send()
    for c in range(4):
        for n in range(7):
            a2a_copy(c, n).wait_send()
        if c >= 2:
            out_copy(c).wait()


def solution(mesh):
    seq_spec = P('dp', 'tp', None, None)
    head_spec = P('dp', None, 'tp', None)
    col_spec = P(None, None, 'tp')
    ff_spec = P(None, None, None, 'tp')
    peers = mesh.shape['tp']

    def local_step(hidden, lengths, choice, keys_one, vals_one, keys_two, vals_two, g_attn, w_q, w_k, w_v, w_o, g_mlp, w_router, w_gate, w_up, w_down):
        rows, pos, heads, head = keys_one.shape
        dim = hidden.shape[1]
        layers, experts, ff = w_down.shape[:3]
        seq = pos * peers
        flat = lambda t: t.reshape(rows * pos * heads, head)
        turn = lambda t: jnp.swapaxes(t, -1, -2)
        wide = experts * ff
        any_spec = pl.BlockSpec(memory_space=pl.ANY)
        cache_shape = jax.ShapeDtypeStruct((rows * head, seq), BF16)
        wqkv_rows = w_q.shape[2] + w_k.shape[2] + 2 * w_v.shape[2]
        scratch = [
            pltpu.VMEM((rows, dim), BF16), pltpu.VMEM((layers, choice.shape[2], rows), jnp.int32),
            pltpu.VMEM((layers, dim), BF16), pltpu.VMEM((layers, dim), BF16),
            pltpu.VMEM((3, rows * pos * heads, head), BF16), pltpu.VMEM((4, heads, pos, rows * head), BF16),
            pltpu.VMEM((4, seq, rows * head), BF16), pltpu.VMEM((2, rows * head, seq), BF16),
            pltpu.VMEM((layers, wqkv_rows, dim), BF16), pltpu.VMEM((layers, w_o.shape[1], dim), BF16),
            pltpu.VMEM((layers, experts, dim), BF16),
            pltpu.VMEM((layers, wide, dim), BF16), pltpu.VMEM((layers, wide, dim), BF16), pltpu.VMEM((layers, wide, dim), BF16),
            pltpu.VMEM((layers, 128, 256), BF16), pltpu.VMEM((layers, rows, 128), F32), pltpu.VMEM((layers, rows, 128), F32),
            pltpu.VMEM((128, seq), F32), pltpu.VMEM((128, 256), F32),
            pltpu.VMEM((CHUNKS, rows, wide // CHUNKS), F32), pltpu.VMEM((layers, rows, wide), BF16),
            pltpu.VMEM((4, rows, dim // 2), BF16), pltpu.VMEM((4, rows, dim // 2), BF16),
            pltpu.VMEM((4, CHIPS, rows, dim // 2), BF16), pltpu.VMEM((4, 2, rows, dim // 2), BF16),
            pltpu.SemaphoreType.DMA((6,)), pltpu.SemaphoreType.DMA((4,)), pltpu.SemaphoreType.DMA((layers, 3, CHUNKS)),
            pltpu.SemaphoreType.DMA((layers, 4)), pltpu.SemaphoreType.DMA((4,)),
            pltpu.SemaphoreType.DMA((4, 7)), pltpu.SemaphoreType.DMA((4, 7)),
            pltpu.SemaphoreType.DMA((4, 5)), pltpu.SemaphoreType.DMA((4, 5)),
        ]
        out = pl.pallas_call(
            kernel,
            name="decode_step",
            out_shape=(jax.ShapeDtypeStruct((rows, dim), BF16),) + (cache_shape,) * 4,
            in_specs=[pl.BlockSpec(memory_space=pltpu.SMEM)] + [any_spec] * 16,
            out_specs=(pl.BlockSpec(memory_space=pltpu.VMEM),) + (any_spec,) * 4,
            scratch_shapes=scratch,
            compiler_params=pltpu.CompilerParams(collective_id=0, has_side_effects=True, vmem_limit_bytes=67043328),
        )(lengths, hidden, turn(choice), flat(keys_one), flat(vals_one), flat(keys_two), flat(vals_two), g_attn, turn(w_q), turn(w_k), turn(w_v), w_o,
          g_mlp, turn(w_router), turn(w_gate).reshape(layers, wide, dim), turn(w_up).reshape(layers, wide, dim), w_down.reshape(layers, wide, dim))
        caches = [jnp.transpose(t.reshape(rows, head, seq), (0, 2, 1))[:, :, None, :] for t in out[1:]]
        return (out[0], *caches)

    return jax.shard_map(local_step, mesh=mesh, in_specs=(P('dp', None), P('dp'), P(None, 'dp', None), seq_spec, seq_spec, seq_spec, seq_spec, P(), col_spec, col_spec, col_spec, P(None, 'tp', None), P(), P(), ff_spec, ff_spec, P(None, None, 'tp', None)), out_specs=(P('dp', None), head_spec, head_spec, head_spec, head_spec), check_vma=False)
```

time: 331 us -> 83.7 us (0.25)
  waiting for transfers between devices: 198 us -> 0 us
  Pallas kernels: 0 us -> 73.7 us
  matrix products: 49.6 us -> 0 us
  starting transfers between devices: 21.9 us -> 0 us
  local copies, waits for them, and re-layouts: 30.4 us -> 9.01 us
  other arithmetic: 14.5 us -> 0 us
  between operations: 14.2 us -> 0.65 us
    psum x4 -> x0, waiting for transfers between devices: 179 us -> none  [the longest x2 93.2 us: decode_layer(): lax.psum(jnp.dot(attn_vec, w_o, preferred_element_type=jnp.float32).astyp...]
    pallas_call x0 -> x1, Pallas kernels: none -> 73.7 us  [local_step(): pl.pallas_call(kernel, name='decode_step', out_shape=(jax.ShapeDtypeStruc...]
    dot_general x18 -> x0, matrix products: 49.6 us -> none  [the longest x2 18.6 us: expert_block(): jnp.einsum('bef,efd->bd', expert_in, w_down, preferred_element_type=jnp.f...]
    all_to_all x4 -> x0, starting transfers between devices: 21.3 us -> none  [local_step(): lax.all_to_all(cache_blk, 'tp', 2, 1, tiled=True)]
    all_to_all x4 -> x0, waiting for transfers between devices: 18.3 us -> none  [local_step(): lax.all_to_all(cache_blk, 'tp', 2, 1, tiled=True)]
    unnamed x40 -> x5, local copies, waits for them, and re-layouts: 26.9 us -> 9.01 us
    select_n x1 -> x0, other arithmetic: 5.13 us -> none  [decode_layer(): val_cache = jnp.where(is_new, val_new[:, None], val_cache)]
    reduce_sum x10 -> x0, other arithmetic: 4 us -> none  [the longest x4 3.24 us: rms_norm(): jnp.mean(tensor_f * tensor_f, axis=-1, keepdims=True) + EPS]
  transfers between devices with their start and end apart: 8 -> 0, of which waited for: 7 -> 0; matrix products, arithmetic and copies ran while one was open for 12% -> 0% of each run, Pallas kernels for 0% -> 0%
where the time goes in v1:
time: 83.7 us; the launch traced here: 83.4 us
  Pallas kernels  73.7 us (88%)
  local copies, waits for them, and re-layouts  9.01 us (11%)
    pallas_call x1, Pallas kernels, local_step(): pl.pallas_call(kernel, name='decode_step', out_shape=(jax.ShapeDtypeStruc...  73.7 us
    unnamed x5, local copies, waits for them, and re-layouts  9.01 us

profile of v1, /device:TPU:113, one launch (start us, length us, event | category | flops | bytes accessed | tf_op | source)
XLA Modules:
  0.0 83.4 jit_solution(14389437412814660074)
XLA Ops:
  0.6 73.7 %decode_step.1 = (bf16[32,1536]{1,0:T(8,128)(2,1)}, bf16[2048,128]{1,0:T(8,128)(2,1)}, bf16[2048,128]{1,0:T(8,128)(2,1)}, bf16[2048,128]{1,0:T(8,128)(2,1)}, bf16[2048,128]{1,0:T(8,128)(2,1)}) custom-call(s32[32]{0:T(128)} %len_s.1, bf16[32,1536]{1,0:T(8,128)(2,1)} %hid_h.1, s32[2,8,32]{2,1,0:T(8,128)} %bitcast.51, bf16[4096,64]{1,0:T(8,128)(2,1)} %bitcast.40, ...), custom_call_target="tpu_custom_call" | custom-call | tf_op jit(solution)/shard_map/decode_step/pallas_call | solution.py:375
  74.3 1.5 %copy.27 = bf16[32,1536]{1,0:T(8,128)(2,1)} copy(bf16[32,1536]{1,0:T(8,128)(2,1)} %get-tuple-element.20) | data formatting | bytes 196608
  75.9 1.9 %copy.28 = bf16[32,128,1,64]{1,3,2,0:T(8,128)(2,1)} copy(bf16[32,128,1,64]{1,3,2,0:T(8,128)(2,1)} %bitcast.47) | data formatting | bytes 1048576
  77.7 1.9 %copy.29 = bf16[32,128,1,64]{1,3,2,0:T(8,128)(2,1)} copy(bf16[32,128,1,64]{1,3,2,0:T(8,128)(2,1)} %bitcast.46) | data formatting | bytes 1048576
  79.6 1.9 %copy.30 = bf16[32,128,1,64]{1,3,2,0:T(8,128)(2,1)} copy(bf16[32,128,1,64]{1,3,2,0:T(8,128)(2,1)} %bitcast.45) | data formatting | bytes 1048576
  81.5 1.9 %copy.31 = bf16[32,128,1,64]{1,3,2,0:T(8,128)(2,1)} copy(bf16[32,128,1,64]{1,3,2,0:T(8,128)(2,1)} %bitcast.44) | data formatting | bytes 1048576

commit v2 on v1

v2 whole, which is shorter than its diff:
```python
import functools

import jax
import jax.numpy as jnp
from jax import lax
from jax.experimental import pallas as pl
from jax.experimental.pallas import tpu as pltpu
from jax.sharding import PartitionSpec as P

EPS = 1e-5
THETA = 1000000.0
MESH = pl.DeviceIdType.MESH
F32 = jnp.float32
BF16 = jnp.bfloat16
CHIPS = 4
OFFSETS = ((2, 0), (2, 1), (1, 0), (3, 0), (1, 1), (3, 1), (0, 1))
CHUNKS = 10


def nt(lhs, rhs):
    return lax.dot_general(lhs, rhs, (((1,), (1,)), ((), ())), preferred_element_type=F32)


def nn(lhs, rhs):
    return jnp.dot(lhs, rhs, preferred_element_type=F32)


def iota(shape, dim):
    return lax.broadcasted_iota(jnp.int32, shape, dim)


def kernel(len_s, hid_h, choice_h, k1_h, v1_h, k2_h, v2_h, ga_h, wq_h, wk_h, wv_h, wo_h, gm_h, wr_h, wg_h, wu_h, wd_h,
           out_hid, ok1, ov1, ok2, ov2,
           hid, choice, ga, gm, xst, sendb, recvb, outst, wqkv, wo, wr, wg, wu, wd,
           qall, kdup, vdup, sc, ov, ubuf, part, d1, shot, fin,
           sem_small, sem_x, sem_w, sem_wqkv, sem_out, ss_a, rs_a, ss_r, rs_r):
    rows, dim = hid.shape
    half = dim // 2
    seq = recvb.shape[1]
    pos = seq // (2 * CHIPS)
    lanes = recvb.shape[2]
    groups = lanes // 256
    head = 64
    experts = wr.shape[1]
    step = wg.shape[1] // CHUNKS

    me = lax.axis_index("tp")
    chip, core = me // 2, lax.rem(me, 2)
    partner = chip * 2 + 1 - core

    def device(dx, flip):
        return lax.rem(chip + dx, CHIPS) * 2 + (1 - core if flip else core)

    def rcopy(src, dst, ssem, rsem, peer):
        return pltpu.make_async_remote_copy(src, dst, ssem, rsem, device_id={"tp": peer}, device_id_type=MESH)

    loads = [pltpu.make_async_copy(src, xst.at[c], sem_x.at[c]) for c, src in enumerate((k1_h, v1_h, k2_h, v2_h))]
    small = [pltpu.make_async_copy(src, dst, sem_small.at[n]) for n, (src, dst) in enumerate(
        ((hid_h, hid), (choice_h, choice), (ga_h, ga), (gm_h, gm), (wr_h, wr), (wo_h, wo)))]

    def qkv_loads(layer):
        nq, nk = wq_h.shape[1], wk_h.shape[1]
        return [pltpu.make_async_copy(src.at[layer], wqkv.at[layer, pl.ds(at, size)], sem_wqkv.at[layer, n])
                for n, (src, at, size) in enumerate(((wq_h, 0, nq), (wk_h, nq, nk), (wv_h, nq + nk, nk), (wv_h, nq + 2 * nk, nk)))]

    loads[0].start()
    barrier = pltpu.get_barrier_semaphore()
    for dx, flip in OFFSETS:
        pl.semaphore_signal(barrier, inc=1, device_id={"tp": device(dx, flip)}, device_id_type=MESH)
    for copy in small[:4]:
        copy.start()
    for copy in qkv_loads(0):
        copy.start()
    loads[1].start()
    loads[2].start()
    loads[3].start()
    for copy in small[4:]:
        copy.start()
    for copy in qkv_loads(1):
        copy.start()

    def w_copy(layer, which, c):
        src, dst = ((wg_h, wg), (wu_h, wu), (wd_h, wd))[which]
        at = pl.ds(pl.multiple_of(c * step, step), step)
        return pltpu.make_async_copy(src.at[layer, at], dst.at[layer, at], sem_w.at[layer, which, c])

    def permute(c):
        i, j = iota((128, 128), 0), iota((128, 128), 1)
        perm = (j == lax.rem(i, 16) * 8 + i // 16).astype(BF16)

        for t in range(groups):
            tiles = [xst[c, slice(t * 512 + n * 128, t * 512 + n * 128 + 128), :] for n in range(4)]
            moved = nn(perm, jnp.concatenate(tiles, axis=1)).astype(BF16)
            sendb[c, :, :, slice(t * 256, t * 256 + 256)] = moved.reshape(8, pos, 256)

    def a2a_copy(c, n):
        peer = device(*OFFSETS[n])
        return rcopy(sendb.at[c, peer], recvb.at[c, pl.ds(pl.multiple_of(me * pos, pos), pos)], ss_a.at[c, n], rs_a.at[c, n], peer)

    def a2a_wait(c):
        for n, (dx, flip) in reversed(list(enumerate(OFFSETS))):
            origin = device(CHIPS - dx, flip)
            rcopy(sendb.at[c, origin], recvb.at[c, pl.ds(pl.multiple_of(origin * pos, pos), pos)], ss_a.at[c, n], rs_a.at[c, n], origin).wait_recv()

    def keep_own(c):
        recvb[c, pl.ds(pl.multiple_of(me * pos, pos), pos), :] = sendb[c, me]

    with jax.named_scope("x0_wait"):
        loads[0].wait()
    for layer in range(2):
        def start_weights(c, _, layer=layer):
            w_copy(layer, 0, c).start()
            w_copy(layer, 1, c).start()
            w_copy(layer, 2, c).start()
            return 0
        lax.fori_loop(0, CHUNKS, start_weights, 0)

    with jax.named_scope("permute0"):
        permute(0)
    with jax.named_scope("barrier"):
        pl.semaphore_wait(barrier, len(OFFSETS))
    for n in range(7):
        a2a_copy(0, n).start()
    with jax.named_scope("permute1"):
        loads[1].wait()
        permute(1)
    for n in range(7):
        a2a_copy(1, n).start()
    keep_own(0)
    keep_own(1)

    lane = iota((rows, 128), 1)
    row = iota((rows, 128), 0)
    len_f = jnp.zeros((rows, 128), F32)
    for b in range(rows):
        len_f = jnp.where(row == b, len_s[b].astype(F32), len_f)
    freq = jnp.exp(lax.rem(lane, 32).astype(F32) * (-2.0 / head * 13.815510557964274))
    angle = len_f * freq
    cos_t, sin_t = jnp.cos(angle), jnp.sin(angle)
    low = lax.rem(lane, head) < head // 2
    left = lane < head

    def rope(x):
        turned = jnp.where(low, -pltpu.roll(x, 96, 1), pltpu.roll(x, 32, 1))
        return (x * cos_t + turned * sin_t).astype(BF16).astype(F32)

    def norm(x, gain):
        scale = lax.rsqrt(jnp.mean(x * x, axis=-1, keepdims=True) + EPS)
        return (x * scale * gain.astype(F32)).astype(BF16)

    def project(layer, x):
        for copy in qkv_loads(layer):
            copy.wait()
        qkv = nt(norm(x, ga[layer:layer + 1, :]), wqkv[layer])
        t0, t1 = rope(qkv[:, :128]), rope(qkv[:, 128:256])
        s0, s1 = pltpu.roll(t0, 64, 1), pltpu.roll(t1, 64, 1)
        q3 = jnp.concatenate([jnp.where(left, t0, s0), jnp.where(left, s0, t0), jnp.where(left, t1, s1)], axis=0).astype(BF16)
        kdup[layer] = jnp.where(left, s1, t1)
        vdup[layer] = qkv[:, 256:384].astype(BF16).astype(F32)
        i, j = iota((128, 96), 0), iota((128, 96), 1)
        slot = lax.rem(i, 16)
        pick = (slot < 12) & (j == lax.rem(slot, 3) * rows + i // 16 * 4 + slot // 3)
        dup = nn(pick.astype(BF16), q3)
        slot2, lane2 = lax.rem(iota((128, 256), 0), 16), iota((128, 256), 1)
        both = jnp.concatenate([dup, dup], axis=1)
        qall[layer] = jnp.where(slot2 // 3 == lane2 // 64, both, 0.0).astype(BF16)

    def place_new(c, t, fresh, layer):
        at = slice(t * 256, t * 256 + 256)
        pos_i, lane_i = iota((seq, 128), 0), iota((seq, 128), 1)
        pieces = []
        for n in range(2):
            first = t * 4 + 2 * n
            where_new = jnp.where(lane_i < head, len_s[first], len_s[first + 1])
            line = jnp.where(lane_i[:1] < head, fresh[layer, first:first + 1, :], fresh[layer, first + 1:first + 2, :])
            old = recvb[c, :, slice(t * 256 + n * 128, t * 256 + n * 128 + 128)].astype(F32)
            pieces.append(jnp.where(pos_i == where_new, line, old))
        tile = jnp.concatenate(pieces, axis=1).astype(BF16)
        recvb[c, :, at] = tile
        return tile

    def attend(layer):
        ck, cv = 2 * layer, 2 * layer + 1
        with jax.named_scope("wait_keys"):
            a2a_wait(ck)

        def scores(t):
            tile = place_new(ck, t, kdup, layer)
            at = slice(t * 16, t * 16 + 16)
            s = nt(qall[layer, at, :], tile) * (head ** -0.5)
            slot, p = iota((16, seq), 0), iota((16, seq), 1)
            limit = jnp.where(slot < 3, len_s[4 * t], jnp.where(slot < 6, len_s[4 * t + 1], jnp.where(slot < 9, len_s[4 * t + 2], len_s[4 * t + 3])))
            sc[at, :] = jnp.where(p <= limit, s, -1e30)
        with jax.named_scope("scores"):
            for t in range(groups):
                scores(t)
        s = sc[...]
        e = jnp.exp(s - jnp.max(s, axis=-1, keepdims=True))
        sc[...] = e / jnp.sum(e, axis=-1, keepdims=True)
        with jax.named_scope("wait_values"):
            a2a_wait(cv)

        def values(t):
            tile = place_new(cv, t, vdup, layer)
            at = slice(t * 16, t * 16 + 16)
            ov[at, :] = nn(sc[at, :].astype(BF16), tile)
        with jax.named_scope("values"):
            for t in range(groups):
                values(t)
        slot2, lane2 = lax.rem(iota((128, 256), 0), 16), iota((128, 256), 1)
        kept = jnp.where(slot2 // 3 == lane2 // 64, ov[...], 0.0)
        both = (kept[:, :128] + kept[:, 128:]).astype(BF16)
        i, j = iota((rows, 128), 0), iota((rows, 128), 1)
        per_head = []
        for r in range(3):
            pick = j == i // 4 * 16 + lax.rem(i, 4) * 3 + r
            got = nn(pick.astype(BF16), both)
            per_head.append(got + pltpu.roll(got, 64, 1))
        return jnp.where(left, per_head[0], per_head[1]).astype(BF16), per_head[2].astype(BF16)[:, :head]

    outs = (ok1, ov1, ok2, ov2)

    def out_copy(c):
        return pltpu.make_async_copy(outst.at[c % 2], outs[c], sem_out.at[c])

    def write_out(c):
        if c >= 2:
            out_copy(c - 2).wait()
        for t in range(groups):
            outst[c % 2, t * 256:(t + 1) * 256, :] = recvb[c, :, t * 256:(t + 1) * 256].T
        out_copy(c).start()

    def cols(which):
        return pl.ds(pl.multiple_of(which * half, half), half)

    def block(which, q, size):
        return pl.ds(pl.multiple_of(which * half + q * size, size), size)

    def all_reduce(r, product, residual, between, parts):
        size = half // parts
        per = shot.shape[2] // parts
        copies = []

        def send(src, dst, kind, q, peer):
            copy = rcopy(src, dst, ss_r.at[r, kind, q], rs_r.at[r, kind, q], peer)
            copy.start()
            copies.append(copy)
            return copy

        def put(ref, q, value):
            for n in range(per):
                ref[q * per + n] = value[:, n * (size // per):(n + 1) * (size // per)].astype(BF16)

        def get(ref, q):
            return jnp.concatenate([ref[q * per + n].astype(F32) for n in range(per)], axis=1)

        swaps = []
        for q in range(parts):
            put(part.at[r], q, product(1 - core, q, size))
            at = pl.ds(q * per, per)
            swaps.append(send(part.at[r, at], d1.at[r, at], 0, q, partner))
        for q in range(parts):
            mine = product(core, q, size)
            with jax.named_scope("swap_wait"):
                swaps[q].wait_recv()
            put(shot.at[r, chip], q, mine + get(d1.at[r], q))
            piece = shot.at[r, chip, pl.ds(q * per, per)]
            for n, dx in enumerate((2, 1, 3)):
                send(piece, piece, 1 + n, q, device(dx, 0))
        with jax.named_scope("between"):
            between()
        for q in range(parts):
            at = pl.ds(q * per, per)
            with jax.named_scope("shot_wait"):
                for n, dx in enumerate((2, 1, 3)):
                    piece = shot.at[r, lax.rem(chip + CHIPS - dx, CHIPS), at]
                    rcopy(piece, piece, ss_r.at[r, 1 + n, q], rs_r.at[r, 1 + n, q], device(dx, 0)).wait_recv()
            total = (get(shot.at[r, 0], q) + get(shot.at[r, 1], q)) + (get(shot.at[r, 2], q) + get(shot.at[r, 3], q))
            put(fin.at[r, core], q, residual(q, size) + total)
            send(fin.at[r, core, at], fin.at[r, core, at], 4, q, partner)
        with jax.named_scope("last_wait"):
            for q in range(parts):
                piece = fin.at[r, 1 - core, pl.ds(q * per, per)]
                rcopy(piece, piece, ss_r.at[r, 4, q], rs_r.at[r, 4, q], partner).wait_recv()
        pieces = [fin[r, h, n].astype(F32) for h in range(2) for n in range(shot.shape[2])]
        return copies, jnp.concatenate(pieces, axis=1)

    def gates(layer, m):
        logits = nt(wr[layer], m)
        e_i = iota((experts, rows), 0)
        chosen = e_i == choice[layer, 0:1, :]
        for n in range(1, choice.shape[1]):
            chosen = chosen | (e_i == choice[layer, n:n + 1, :])
        top = jnp.max(jnp.where(chosen, logits, -3e38), axis=0, keepdims=True)
        weight = jnp.where(chosen, jnp.exp(jnp.where(chosen, logits - top, 0.0)), 0.0)
        return (weight / jnp.sum(weight, axis=0, keepdims=True)).T

    def wait_weights(layer):
        def body(c, _):
            for which in range(3):
                w_copy(layer, which, c).wait()
            return 0
        lax.fori_loop(0, CHUNKS, body, 0)

    def experts_up(layer, m):
        gate = gates(layer, m)
        pairs = step // 128
        for c in range(CHUNKS):
            at = slice(c * step, (c + 1) * step)
            g = nt(m, wg[layer, at, :])
            up = nt(m, wu[layer, at, :])
            wide = jnp.concatenate([jnp.where(left, gate[:, 2 * n:2 * n + 1], gate[:, 2 * n + 1:2 * n + 2]) for n in range(c * pairs, (c + 1) * pairs)], axis=1)
            ubuf[layer, :, at] = (jax.nn.silu(g) * up * wide).astype(BF16)

    for copy in small:
        copy.wait()
    x = hid[...].astype(F32)
    with jax.named_scope("project"):
        project(0, x)
    with jax.named_scope("permute23"):
        loads[2].wait()
        permute(2)
        loads[3].wait()
        permute(3)
        keep_own(2)
        keep_own(3)

    pending = []
    for layer in range(2):
        if layer:
            with jax.named_scope("project"):
                project(layer, x)
        first, second = attend(layer)
        n1 = first.shape[1]

        def out_product(which, q, size, layer=layer, first=first, second=second, n1=n1):
            at = block(which, q, size)
            return nn(first, wo[layer, :n1, at]) + nn(second, wo[layer, n1:, at])

        def between_attn(layer=layer):
            if layer == 0:
                for c in (2, 3):
                    for n in range(7):
                        a2a_copy(c, n).start()
            write_out(2 * layer)
            write_out(2 * layer + 1)
            wait_weights(layer)

        def residual_attn(q, size, layer=layer):
            if layer:
                return jnp.concatenate([fin[2 * layer - 1, core, n].astype(F32) for n in range(shot.shape[2])], axis=1)
            return hid[:, block(core, q, size)].astype(F32)

        copies, x = all_reduce(2 * layer, out_product, residual_attn, between_attn, 1)
        pending += copies
        m = norm(x, gm[layer:layer + 1, :])
        with jax.named_scope("up"):
            experts_up(layer, m)

        def down_product(which, q, size, layer=layer):
            with jax.named_scope("down"):
                return nn(ubuf[layer], wd[layer, :, block(which, q, size)])

        def residual_moe(q, size, layer=layer):
            return fin[2 * layer, core, q].astype(F32)

        copies, x = all_reduce(2 * layer + 1, down_product, residual_moe, lambda: None, 2)
        pending += copies
    out_hid[...] = x.astype(BF16)

    with jax.named_scope("tail"):
        for copy in pending:
            copy.wait_send()
        for c in range(4):
            for n in range(7):
                a2a_copy(c, n).wait_send()
            if c >= 2:
                out_copy(c).wait()


def finish(*refs):
    n = (len(refs) - 2) // 3
    srcs, dsts, bufs, in_sem, out_sem = refs[:n], refs[n:2 * n], refs[2 * n:3 * n], refs[-2], refs[-1]
    into = [pltpu.make_async_copy(srcs[i], bufs[i], in_sem.at[i]) for i in range(n)]
    out = [pltpu.make_async_copy(bufs[i], dsts[i], out_sem.at[i]) for i in range(n)]
    for copy in into:
        copy.start()
    for i in range(n):
        into[i].wait()
        out[i].start()
    for copy in out:
        copy.wait()


def solution(mesh):
    seq_spec = P('dp', 'tp', None, None)
    head_spec = P('dp', None, 'tp', None)
    col_spec = P(None, None, 'tp')
    ff_spec = P(None, None, None, 'tp')
    peers = mesh.shape['tp']

    def local_step(hidden, lengths, choice, keys_one, vals_one, keys_two, vals_two, g_attn, w_q, w_k, w_v, w_o, g_mlp, w_router, w_gate, w_up, w_down):
        rows, pos, heads, head = keys_one.shape
        dim = hidden.shape[1]
        layers, experts, ff = w_down.shape[:3]
        seq = pos * peers
        flat = lambda t: t.reshape(rows * pos * heads, head)
        turn = lambda t: jnp.swapaxes(t, -1, -2)
        wide = experts * ff
        any_spec = pl.BlockSpec(memory_space=pl.ANY)
        cache_shape = jax.ShapeDtypeStruct((rows * head, seq), BF16)
        wqkv_rows = w_q.shape[2] + w_k.shape[2] + 2 * w_v.shape[2]
        scratch = [
            pltpu.VMEM((rows, dim), BF16), pltpu.VMEM((layers, choice.shape[2], rows), jnp.int32),
            pltpu.VMEM((layers, dim), BF16), pltpu.VMEM((layers, dim), BF16),
            pltpu.VMEM((4, rows * pos * heads, head), BF16), pltpu.VMEM((4, heads, pos, rows * head), BF16),
            pltpu.VMEM((4, seq, rows * head), BF16), pltpu.VMEM((2, rows * head, seq), BF16),
            pltpu.VMEM((layers, wqkv_rows, dim), BF16), pltpu.VMEM((layers, w_o.shape[1], dim), BF16),
            pltpu.VMEM((layers, experts, dim), BF16),
            pltpu.VMEM((layers, wide, dim), BF16), pltpu.VMEM((layers, wide, dim), BF16), pltpu.VMEM((layers, wide, dim), BF16),
            pltpu.VMEM((layers, 128, 256), BF16), pltpu.VMEM((layers, rows, 128), F32), pltpu.VMEM((layers, rows, 128), F32),
            pltpu.VMEM((128, seq), F32), pltpu.VMEM((128, 256), F32),
            pltpu.VMEM((layers, rows, wide), BF16),
            pltpu.VMEM((4, 2, rows, dim // 4), BF16), pltpu.VMEM((4, 2, rows, dim // 4), BF16),
            pltpu.VMEM((4, CHIPS, 2, rows, dim // 4), BF16), pltpu.VMEM((4, 2, 2, rows, dim // 4), BF16),
            pltpu.SemaphoreType.DMA((6,)), pltpu.SemaphoreType.DMA((4,)), pltpu.SemaphoreType.DMA((layers, 3, CHUNKS)),
            pltpu.SemaphoreType.DMA((layers, 4)), pltpu.SemaphoreType.DMA((4,)),
            pltpu.SemaphoreType.DMA((4, 7)), pltpu.SemaphoreType.DMA((4, 7)),
            pltpu.SemaphoreType.DMA((4, 5, 2)), pltpu.SemaphoreType.DMA((4, 5, 2)),
        ]
        out = pl.pallas_call(
            kernel,
            name="decode_step",
            out_shape=(jax.ShapeDtypeStruct((rows, dim), BF16),) + (cache_shape,) * 4,
            in_specs=[pl.BlockSpec(memory_space=pltpu.SMEM)] + [any_spec] * 16,
            out_specs=(pl.BlockSpec(memory_space=pltpu.VMEM),) + (any_spec,) * 4,
            scratch_shapes=scratch,
            compiler_params=pltpu.CompilerParams(collective_id=0, has_side_effects=True, vmem_limit_bytes=67043328),
        )(lengths, hidden, turn(choice), flat(keys_one), flat(vals_one), flat(keys_two), flat(vals_two), g_attn, turn(w_q), turn(w_k), turn(w_v), w_o,
          g_mlp, turn(w_router), turn(w_gate).reshape(layers, wide, dim), turn(w_up).reshape(layers, wide, dim), w_down.reshape(layers, wide, dim))
        out = pl.pallas_call(
            finish,
            name="finish",
            out_shape=[jax.ShapeDtypeStruct(t.shape, t.dtype) for t in out],
            in_specs=[any_spec] * len(out),
            out_specs=[any_spec] * len(out),
            scratch_shapes=[pltpu.VMEM(t.shape, t.dtype) for t in out] + [pltpu.SemaphoreType.DMA((len(out),))] * 2,
        )(*out)
        caches = [jnp.transpose(t.reshape(rows, head, seq), (0, 2, 1))[:, :, None, :] for t in out[1:]]
        return (out[0], *caches)

    return jax.shard_map(local_step, mesh=mesh, in_specs=(P('dp', None), P('dp'), P(None, 'dp', None), seq_spec, seq_spec, seq_spec, seq_spec, P(), col_spec, col_spec, col_spec, P(None, 'tp', None), P(), P(), ff_spec, ff_spec, P(None, None, 'tp', None)), out_specs=(P('dp', None), head_spec, head_spec, head_spec, head_spec), check_vma=False)
```

time: 83.7 us -> 65.5 us (0.78)
  Pallas kernels: 73.7 us -> 64.6 us
  local copies, waits for them, and re-layouts: 9.01 us -> 0 us
    pallas_call x1, Pallas kernels: 73.7 us -> 62.1 us  [local_step(): pl.pallas_call(kernel, name='decode_step', out_shape=(jax.ShapeDtypeStruc...]
    unnamed x5 -> x0, local copies, waits for them, and re-layouts: 9.01 us -> none
    pallas_call x0 -> x1, Pallas kernels: none -> 2.5 us  [local_step(): pl.pallas_call(finish, name='finish', out_shape=[jax.ShapeDtypeStruct(t.s...]
where the time goes in v2:
time: 65.5 us; the launch traced here: 65.4 us
  Pallas kernels  64.6 us (99%)
  between operations  0.81 us (1%)
    pallas_call x1, Pallas kernels, local_step(): pl.pallas_call(kernel, name='decode_step', out_shape=(jax.ShapeDtypeStruc...  62.1 us
    pallas_call x1, Pallas kernels, local_step(): pl.pallas_call(finish, name='finish', out_shape=[jax.ShapeDtypeStruct(t.s...  2.5 us

profile of v2, /device:TPU:113, one launch (start us, length us, event | category | flops | bytes accessed | tf_op | source)
XLA Modules:
  0.0 65.4 jit_solution(7749850153034008215)
XLA Ops:
  0.6 62.1 %decode_step.1 = (bf16[32,1536]{1,0:T(8,128)(2,1)}, bf16[2048,128]{1,0:T(8,128)(2,1)}, bf16[2048,128]{1,0:T(8,128)(2,1)}, bf16[2048,128]{1,0:T(8,128)(2,1)}, bf16[2048,128]{1,0:T(8,128)(2,1)}) custom-call(s32[32]{0:T(128)} %len_s.1, bf16[32,1536]{1,0:T(8,128)(2,1)} %hid_h.1, s32[2,8,32]{2,1,0:T(8,128)} %bitcast.47, bf16[4096,64]{1,0:T(8,128)(2,1)} %bitcast.40, ...), custom_call_target="tpu_custom_call" | custom-call | tf_op jit(solution)/shard_map/decode_step/pallas_call | solution.py:431
  62.7 2.5 %finish.1 = (bf16[32,1536]{1,0:T(8,128)(2,1)}, bf16[2048,128]{1,0:T(8,128)(2,1)}, bf16[2048,128]{1,0:T(8,128)(2,1)}, bf16[2048,128]{1,0:T(8,128)(2,1)}, bf16[2048,128]{1,0:T(8,128)(2,1)}) custom-call(bf16[32,1536]{1,0:T(8,128)(2,1)} %get-tuple-element.15.refs_0_, bf16[2048,128]{1,0:T(8,128)(2,1)} %get-tuple-element.16.refs_1_, ...), custom_call_target="tpu_custom_call" | custom-call | tf_op jit(solution)/shard_map/finish/pallas_call | solution.py:441

commit v3 on v2

v3 whole, which is shorter than its diff:
```python
import functools

import jax
import jax.numpy as jnp
from jax import lax
from jax.experimental import pallas as pl
from jax.experimental.pallas import tpu as pltpu
from jax.sharding import PartitionSpec as P

EPS = 1e-5
THETA = 1000000.0
MESH = pl.DeviceIdType.MESH
F32 = jnp.float32
BF16 = jnp.bfloat16
LANES, WIDE, TILE, HEAD = 128, 256, 16, 64
CHIPS = 4
OFFSETS = ((2, 0), (2, 1), (1, 0), (3, 0), (1, 1), (3, 1), (0, 1))
def units(cache, *which):
    pairs = ((0,), (1,), (2, 3), (4, 5), (6,))
    return [(cache, n) for k in which for n in pairs[k]]


WINDOWS = (
    units(2, 2),
    units(2, 4, 0) + units(3, 4),
    [],
    units(2, 1),
    units(2, 3) + units(3, 0, 1, 2, 3),
    units(0, 4, 0, 1, 2) + units(1, 4),
    units(0, 3) + units(1, 0, 1, 2, 3),
)
CHUNKS = 10


def nt(lhs, rhs):
    return lax.dot_general(lhs, rhs, (((1,), (1,)), ((), ())), preferred_element_type=F32)


def nn(lhs, rhs):
    return jnp.dot(lhs, rhs, preferred_element_type=F32)


def iota(shape, dim):
    return lax.broadcasted_iota(jnp.int32, shape, dim)


def kernel(len_h, hid_h, choice_h, k1_h, v1_h, k2_h, v2_h, ga_h, wq_h, wk_h, wv_h, wo_h, gm_h, wr_h, wg_h, wu_h, wd_h,
           out_hid, ok1, ov1, ok2, ov2,
           len_s, hid, choice, ga, gm, xst, sendb, recvb, wqkv, wo, wr, wg, wu, wd,
           qall, kdup, vdup, sc, ov, ubuf, part, d1, shot, fin, qrecv, psend, precv,
           sem_small, sem_x, sem_w, sem_wqkv, ss_a, rs_a, ss_r, rs_r, ss_q, rs_q, ss_p, rs_p):
    rows, dim = hid.shape
    half = dim // 2
    seq = recvb.shape[1]
    pos = seq // (2 * CHIPS)
    lanes = recvb.shape[2]
    groups = lanes // WIDE
    head = HEAD
    experts = wr.shape[1]
    step = wg.shape[1] // CHUNKS

    me = lax.axis_index("tp")
    chip, core = me // 2, lax.rem(me, 2)
    partner = chip * 2 + 1 - core

    def device(dx, flip):
        return lax.rem(chip + dx, CHIPS) * 2 + (1 - core if flip else core)

    def rcopy(src, dst, ssem, rsem, peer):
        return pltpu.make_async_remote_copy(src, dst, ssem, rsem, device_id={"tp": peer}, device_id_type=MESH)

    def drain(ref, sem):
        pltpu.make_async_copy(ref, ref, sem).wait()

    loads = [pltpu.make_async_copy(src, xst.at[c], sem_x.at[c]) for c, src in enumerate((k1_h, v1_h, k2_h, v2_h))]
    small = [pltpu.make_async_copy(src, dst, sem_small.at[n]) for n, (src, dst) in enumerate(
        ((hid_h, hid), (len_h, len_s), (ga_h, ga), (gm_h, gm), (choice_h, choice), (wr_h, wr), (wo_h, wo)))]

    def qkv_loads(layer):
        nq, nk = wq_h.shape[1], wk_h.shape[1]
        return [pltpu.make_async_copy(src.at[layer], wqkv.at[layer, pl.ds(at, size)], sem_wqkv.at[layer])
                for src, at, size in ((wq_h, 0, nq), (wk_h, nq, nk), (wv_h, nq + nk, nk), (wv_h, nq + 2 * nk, nk))]

    small[0].start()
    for copy in qkv_loads(0):
        copy.start()
    for copy in small[1:4]:
        copy.start()
    barrier = pltpu.get_barrier_semaphore()
    for dx, flip in OFFSETS:
        pl.semaphore_signal(barrier, inc=1, device_id={"tp": device(dx, flip)}, device_id_type=MESH)
    for c in (2, 0, 1, 3):
        loads[c].start()
    for copy in small[4:]:
        copy.start()
    for copy in qkv_loads(1):
        copy.start()

    def w_copy(layer, which, c):
        src, dst = ((wg_h, wg), (wu_h, wu), (wd_h, wd))[which]
        at = pl.ds(pl.multiple_of(c * step, step), step)
        return pltpu.make_async_copy(src.at[layer, at], dst.at[layer, at], sem_w.at[layer, which])

    def permute(c):
        i, j = iota((LANES, LANES), 0), iota((LANES, LANES), 1)
        perm = (j == lax.rem(i, TILE) * 8 + i // TILE).astype(BF16)

        for t in range(groups):
            tiles = [xst[c, slice(t * 512 + n * LANES, t * 512 + n * LANES + LANES), :] for n in range(4)]
            moved = nn(perm, jnp.concatenate(tiles, axis=1)).astype(BF16)
            sendb[c, :, :, slice(t * WIDE, t * WIDE + WIDE)] = moved.reshape(8, pos, WIDE)

    def a2a_copy(c, n):
        peer = device(*OFFSETS[n])
        return rcopy(sendb.at[c, peer], recvb.at[c, pl.ds(pl.multiple_of(me * pos, pos), pos)], ss_a.at[c], rs_a.at[c], peer)

    def a2a_wait(c):
        drain(recvb.at[c, pl.ds(0, len(OFFSETS) * pos)], rs_a.at[c])

    def keep_own(c):
        recvb[c, pl.ds(pl.multiple_of(me * pos, pos), pos), :] = sendb[c, me]

    for layer in range(2):
        def start_weights(c, _, layer=layer):
            w_copy(layer, 0, c).start()
            w_copy(layer, 1, c).start()
            w_copy(layer, 2, c).start()
            return 0
        lax.fori_loop(0, CHUNKS, start_weights, 0)

    with jax.named_scope("small_wait"):
        for copy in small[:4]:
            copy.wait()
    lane = iota((rows, LANES), 1)
    row = iota((rows, LANES), 0)
    len_f = jnp.zeros((rows, LANES), F32)
    for b in range(rows):
        len_f = jnp.where(row == b, len_s[b].astype(F32), len_f)
    freq = jnp.exp(lax.rem(lane, 32).astype(F32) * (-2.0 / head * 13.815510557964274))
    angle = len_f * freq
    cos_t, sin_t = jnp.cos(angle), jnp.sin(angle)
    low = lax.rem(lane, head) < head // 2
    left = lane < head

    def rope(x):
        turned = jnp.where(low, -pltpu.roll(x, 96, 1), pltpu.roll(x, 32, 1))
        return (x * cos_t + turned * sin_t).astype(BF16).astype(F32)

    def norm(x, gain):
        scale = lax.rsqrt(jnp.mean(x * x, axis=-1, keepdims=True) + EPS)
        return (x * scale * gain.astype(F32)).astype(BF16)

    def project(layer, x):
        drain(wqkv.at[layer], sem_wqkv.at[layer])
        qkv = nt(norm(x, ga[layer:layer + 1, :]), wqkv[layer])
        t0, t1 = rope(qkv[:, :LANES]), rope(qkv[:, LANES:WIDE])
        s0, s1 = pltpu.roll(t0, HEAD, 1), pltpu.roll(t1, HEAD, 1)
        q3 = jnp.concatenate([jnp.where(left, t0, s0), jnp.where(left, s0, t0), jnp.where(left, t1, s1)], axis=0).astype(BF16)
        kdup[layer] = jnp.where(left, s1, t1)
        vdup[layer] = qkv[:, WIDE:384].astype(BF16).astype(F32)
        return q3

    def block_queries(q3):
        i, j = iota((LANES, 96), 0), iota((LANES, 96), 1)
        slot = lax.rem(i, TILE)
        pick = (slot < 12) & (j == lax.rem(slot, 3) * rows + i // TILE * 4 + slot // 3)
        dup = nn(pick.astype(BF16), q3)
        slot2, lane2 = lax.rem(iota((LANES, WIDE), 0), TILE), iota((LANES, WIDE), 1)
        both = jnp.concatenate([dup, dup], axis=1)
        qall[...] = jnp.where(slot2 // 3 == lane2 // HEAD, both, 0.0).astype(BF16)

    hb = rows // 2
    prow, plane = iota((hb * 4, LANES), 0), iota((hb * 4, LANES), 1)
    pleft = plane < head

    def pack(table, cells):
        width = table.shape[0]
        i, j = iota((hb * 4, width), 0), iota((hb * 4, width), 1)
        low_half = nn(cells(i, j, 0).astype(BF16), table)
        high_half = nn(cells(i, j, hb).astype(BF16), table)
        return jnp.where(pleft, low_half, high_half)

    def pack_queries(q3):
        return pack(q3, lambda i, j, b0: (lax.rem(i, 4) < 3) & (j == lax.rem(i, 4) * rows + i // 4 + b0))

    def pack_fresh(table):
        return pack(table.astype(BF16), lambda i, j, b0: j == i // 4 + b0)

    def to_all(n, src, dst, ssem, rsem):
        return rcopy(src, dst, ssem, rsem, device(*OFFSETS[n]))

    def q_copy(n):
        return to_all(n, qrecv.at[me], qrecv.at[me], ss_q, rs_q)

    def p_copy(n):
        return to_all(n, psend.at[device(*OFFSETS[n])], precv.at[me], ss_p, rs_p)

    def seven(ref):
        return ref.at[pl.ds(0, len(OFFSETS))]

    def local_attend():
        row_i, lane_i = iota((LANES, LANES), 0), iota((LANES, LANES), 1)
        wide_row, wide_lane = iota((LANES, WIDE), 0), iota((LANES, WIDE), 1)
        own_head = row_i // TILE == lax.rem(lane_i, 8)
        where_pos = me * pos + lane_i // 8
        in_group = lax.rem(row_i, TILE) // 4
        slot = lax.rem(row_i, 4)
        diagonal = wide_lane // head == lax.rem(wide_row, TILE) // 4
        half_lane = lane_i < head
        lane_in = lax.rem(lane_i, head)
        done = []
        for t in range(groups):
            at = slice(t % 4 * TILE, t % 4 * TILE + TILE)
            q = qrecv[:, at, :].reshape(LANES, LANES).astype(F32)
            q = jnp.where(half_lane if t < 4 else ~half_lane, q, 0.0)
            q = q + pltpu.roll(q, HEAD, 1)
            q = jnp.where(diagonal, jnp.concatenate([q, q], axis=1), 0.0).astype(BF16)
            keys = jnp.concatenate([xst[0, b * LANES:(b + 1) * LANES, :] for b in range(4 * t, 4 * t + 4)], axis=1)
            vals = jnp.concatenate([xst[1, b * LANES:(b + 1) * LANES, :] for b in range(4 * t, 4 * t + 4)], axis=1)
            s = nt(q, keys) * (head ** -0.5)
            limit = jnp.where(in_group == 0, len_s[4 * t], jnp.where(in_group == 1, len_s[4 * t + 1], jnp.where(in_group == 2, len_s[4 * t + 2], len_s[4 * t + 3])))
            valid = own_head & (where_pos < limit)
            s = jnp.where(valid, s, -1e30)
            top = jnp.max(s, axis=-1, keepdims=True)
            p = jnp.where(valid, jnp.exp(s - top), 0.0)
            total = jnp.sum(p, axis=-1, keepdims=True)
            o = jnp.where(diagonal, nn(p.astype(BF16), vals), 0.0)
            o = o[:, :LANES] + o[:, LANES:]
            o = o + pltpu.roll(o, HEAD, 1)
            stat = jnp.where(slot == 3, 0.0, jnp.where(lane_in == slot, top, jnp.where(lane_in == slot + 3, total, 0.0)))
            stat = pltpu.roll(stat, 1, 0) + pltpu.roll(stat, 2, 0) + pltpu.roll(stat, 3, 0)
            done.append(jnp.where(slot == 3, stat, o))
            if t >= 4:
                psend[:, at, :] = jnp.where(half_lane, done[t - 4], done[t]).reshape(8, TILE, LANES)

    def half_sum(x):
        low_half = jnp.sum(jnp.where(pleft, x, 0.0), axis=-1, keepdims=True)
        high_half = jnp.sum(jnp.where(pleft, 0.0, x), axis=-1, keepdims=True)
        return jnp.where(pleft, low_half, high_half)

    def merge(queries, fresh_k, fresh_v):
        slot, lane_in = lax.rem(prow, 4), lax.rem(plane, head)
        n_rows = prow.shape[0]
        parts = []
        for n in range(2 * CHIPS):
            x = precv[n]
            stat = jnp.where(slot == 0, pltpu.roll(x, n_rows - 3, 0), jnp.where(slot == 1, pltpu.roll(x, n_rows - 2, 0), pltpu.roll(x, n_rows - 1, 0)))
            parts.append((half_sum(jnp.where(lane_in == slot, stat, 0.0)), half_sum(jnp.where(lane_in == slot + 3, stat, 0.0)), x))
        own = half_sum(queries * fresh_k) * (head ** -0.5)
        top = own
        for m, _, _ in parts:
            top = jnp.maximum(top, m)
        weight = jnp.exp(own - top)
        den, num = weight, weight * fresh_v
        for m, total, o in parts:
            weight = jnp.exp(m - top)
            den += weight * total
            num += weight * o
        o = jnp.where(slot == 3, 0.0, num / den).astype(BF16)
        i, j = iota((rows, n_rows), 0), iota((rows, n_rows), 1)
        kept = left == (row < hb)
        per_head = []
        for r in range(3):
            got = jnp.where(kept, nn((j == lax.rem(i, hb) * 4 + r).astype(BF16), o), 0.0)
            per_head.append(got + pltpu.roll(got, HEAD, 1))
        return jnp.where(left, per_head[0], per_head[1]).astype(BF16), per_head[2].astype(BF16)[:, :head]

    def place_new(c, t, fresh, layer):
        at = slice(t * WIDE, t * WIDE + WIDE)
        pos_i, lane_i = iota((seq, LANES), 0), iota((seq, LANES), 1)
        pieces = []
        for n in range(2):
            first = t * 4 + 2 * n
            where_new = jnp.where(lane_i < head, len_s[first], len_s[first + 1])
            line = jnp.where(lane_i[:1] < head, fresh[layer, first:first + 1, :], fresh[layer, first + 1:first + 2, :])
            old = recvb[c, :, slice(t * WIDE + n * LANES, t * WIDE + n * LANES + LANES)].astype(F32)
            pieces.append(jnp.where(pos_i == where_new, line, old))
        tile = jnp.concatenate(pieces, axis=1).astype(BF16)
        recvb[c, :, at] = tile
        return tile

    def attend(layer):
        ck, cv = 2 * layer, 2 * layer + 1
        with jax.named_scope("wait_keys"):
            a2a_wait(ck)

        def scores(t):
            tile = place_new(ck, t, kdup, layer)
            at = slice(t * TILE, t * TILE + TILE)
            s = nt(qall[at, :], tile) * (head ** -0.5)
            slot, p = iota((TILE, seq), 0), iota((TILE, seq), 1)
            limit = jnp.where(slot < 3, len_s[4 * t], jnp.where(slot < 6, len_s[4 * t + 1], jnp.where(slot < 9, len_s[4 * t + 2], len_s[4 * t + 3])))
            sc[at, :] = jnp.where(p <= limit, s, -1e30)
        with jax.named_scope("scores"):
            for t in range(groups):
                scores(t)
        s = sc[...]
        e = jnp.exp(s - jnp.max(s, axis=-1, keepdims=True))
        sc[...] = e / jnp.sum(e, axis=-1, keepdims=True)
        with jax.named_scope("wait_values"):
            a2a_wait(cv)

        def values(t):
            tile = place_new(cv, t, vdup, layer)
            at = slice(t * TILE, t * TILE + TILE)
            ov[at, :] = nn(sc[at, :].astype(BF16), tile)
        with jax.named_scope("values"):
            for t in range(groups):
                values(t)
        slot2, lane2 = lax.rem(iota((LANES, WIDE), 0), TILE), iota((LANES, WIDE), 1)
        kept = jnp.where(slot2 // 3 == lane2 // HEAD, ov[...], 0.0)
        both = (kept[:, :LANES] + kept[:, LANES:]).astype(BF16)
        i, j = iota((rows, LANES), 0), iota((rows, LANES), 1)
        per_head = []
        for r in range(3):
            pick = j == i // 4 * TILE + lax.rem(i, 4) * 3 + r
            got = nn(pick.astype(BF16), both)
            per_head.append(got + pltpu.roll(got, HEAD, 1))
        return jnp.where(left, per_head[0], per_head[1]).astype(BF16), per_head[2].astype(BF16)[:, :head]

    outs = (ok1, ov1, ok2, ov2)

    def write_out(c):
        for t in range(groups):
            outs[c][t * WIDE:(t + 1) * WIDE, :] = recvb[c, :, t * WIDE:(t + 1) * WIDE].T

    def cols(which):
        return pl.ds(pl.multiple_of(which * half, half), half)

    def block(which, q, size):
        return pl.ds(pl.multiple_of(which * half + q * size, size), size)

    def all_reduce(r, product, residual, between, parts, window):
        size = half // parts
        per = shot.shape[2] // parts

        def send(ref, dst, ssem, rsem, peer):
            rcopy(ref, dst, ss_r.at[r, ssem], rs_r.at[r, rsem], peer).start()

        def put(ref, q, value):
            for n in range(per):
                ref[q * per + n] = value[:, n * (size // per):(n + 1) * (size // per)].astype(BF16)

        def get(ref, q):
            return jnp.concatenate([ref[q * per + n].astype(F32) for n in range(per)], axis=1)

        for q in range(parts):
            put(part.at[r], q, product(1 - core, q, size))
            at = pl.ds(q * per, per)
            send(part.at[r, at], d1.at[r, at], 0, q, partner)
        for q in range(parts):
            mine = product(core, q, size)
            with jax.named_scope("swap_wait"):
                drain(d1.at[r, pl.ds(q * per, per)], rs_r.at[r, q])
            put(shot.at[r, chip], q, mine + get(d1.at[r], q))
            piece = shot.at[r, chip, pl.ds(q * per, per)]
            for dx in (2, 1, 3):
                send(piece, piece, 1, 2 + q, device(dx, 0))
        with jax.named_scope("between"):
            between()
        for q in range(parts):
            at = pl.ds(q * per, per)
            with jax.named_scope("shot_wait"):
                drain(shot.at[r, pl.ds(0, CHIPS - 1), at], rs_r.at[r, 2 + q])
            total = (get(shot.at[r, 0], q) + get(shot.at[r, 1], q)) + (get(shot.at[r, 2], q) + get(shot.at[r, 3], q))
            put(fin.at[r, core], q, residual(q, size) + total)
            send(fin.at[r, core, at], fin.at[r, core, at], 0, 4, partner)
        send_caches(window)
        with jax.named_scope("last_wait"):
            drain(fin.at[r, 1 - core], rs_r.at[r, 4])
        pieces = [fin[r, h, n].astype(F32) for h in range(2) for n in range(shot.shape[2])]
        return jnp.concatenate(pieces, axis=1)

    def gates(layer, m):
        logits = nt(wr[layer], m)
        e_i = iota((experts, rows), 0)
        chosen = e_i == choice[layer, 0:1, :]
        for n in range(1, choice.shape[1]):
            chosen = chosen | (e_i == choice[layer, n:n + 1, :])
        top = jnp.max(jnp.where(chosen, logits, -3e38), axis=0, keepdims=True)
        weight = jnp.where(chosen, jnp.exp(jnp.where(chosen, logits - top, 0.0)), 0.0)
        return (weight / jnp.sum(weight, axis=0, keepdims=True)).T

    def wait_weights(layer):
        for which, ref in enumerate((wg, wu, wd)):
            drain(ref.at[layer], sem_w.at[layer, which])

    def experts_up(layer, m):
        gate = gates(layer, m)
        pairs = step // LANES
        for c in range(CHUNKS):
            at = slice(c * step, (c + 1) * step)
            g = nt(m, wg[layer, at, :])
            up = nt(m, wu[layer, at, :])
            wide = jnp.concatenate([jnp.where(left, gate[:, 2 * n:2 * n + 1], gate[:, 2 * n + 1:2 * n + 2]) for n in range(c * pairs, (c + 1) * pairs)], axis=1)
            ubuf[:, at] = (jax.nn.silu(g) * up * wide).astype(BF16)

    def send_caches(wanted):
        for c, n in wanted:
            a2a_copy(c, n).start()

    x = hid[...].astype(F32)
    with jax.named_scope("project"):
        q3 = project(0, x)
        queries = pack_queries(q3)
        fresh_k, fresh_v = pack_fresh(kdup[0]), pack_fresh(vdup[0])
        qrecv[me] = queries.astype(BF16)
    with jax.named_scope("barrier"):
        pl.semaphore_wait(barrier, len(OFFSETS))
    for n in range(7):
        q_copy(n).start()
    with jax.named_scope("permute2"):
        loads[2].wait()
        permute(2)
    send_caches(WINDOWS[0])
    with jax.named_scope("permute_rest"):
        for copy in small[4:]:
            copy.wait()
        for c in (3, 0, 1):
            loads[c].wait()
            permute(c)
        for c in range(4):
            keep_own(c)
    with jax.named_scope("q_wait"):
        drain(seven(qrecv), rs_q)
    send_caches(WINDOWS[1])
    with jax.named_scope("local_attend"):
        local_attend()
    for n in range(7):
        p_copy(n).start()
    precv[me] = psend[me]
    send_caches(WINDOWS[2])
    with jax.named_scope("p_wait"):
        drain(seven(precv), rs_p)
    send_caches(WINDOWS[3])
    with jax.named_scope("merge"):
        first, second = merge(queries, fresh_k, fresh_v)

    for layer in range(2):
        if layer:
            with jax.named_scope("project"):
                block_queries(project(layer, x))
            first, second = attend(layer)
        n1 = first.shape[1]

        def out_product(which, q, size, layer=layer, first=first, second=second, n1=n1):
            at = block(which, q, size)
            return nn(first, wo[layer, :n1, at]) + nn(second, wo[layer, n1:, at])

        def between_attn(layer=layer):
            if layer:
                write_out(2)
                write_out(3)
            wait_weights(layer)

        def between_moe(layer=layer):
            if layer:
                for c, fresh in ((0, kdup), (1, vdup)):
                    a2a_wait(c)
                    for t in range(groups):
                        place_new(c, t, fresh, 0)
                    write_out(c)

        def residual_attn(q, size, layer=layer):
            if layer:
                return jnp.concatenate([fin[2 * layer - 1, core, n].astype(F32) for n in range(shot.shape[2])], axis=1)
            return hid[:, block(core, q, size)].astype(F32)

        x = all_reduce(2 * layer, out_product, residual_attn, between_attn, 1, WINDOWS[4 + 2 * layer])
        m = norm(x, gm[layer:layer + 1, :])
        with jax.named_scope("up"):
            experts_up(layer, m)

        def down_product(which, q, size, layer=layer):
            with jax.named_scope("down"):
                return nn(ubuf[...], wd[layer, :, block(which, q, size)])

        def residual_moe(q, size, layer=layer):
            return fin[2 * layer, core, q].astype(F32)

        x = all_reduce(2 * layer + 1, down_product, residual_moe, between_moe, 2, () if layer else WINDOWS[5])
    out_hid[...] = x.astype(BF16)

    with jax.named_scope("tail"):
        for r in range(4):
            drain(shot.at[r, pl.ds(0, 2)], ss_r.at[r, 0])
            drain(shot.at[r, pl.ds(0, CHIPS - 1)], ss_r.at[r, 1])
        drain(seven(qrecv), ss_q)
        drain(seven(psend), ss_p)
        for c in range(4):
            drain(sendb.at[c, pl.ds(0, len(OFFSETS))], ss_a.at[c])


def finish(*refs):
    n = len(refs) // 2
    copies = [pltpu.make_async_copy(refs[i], refs[n + i], refs[-1].at[i]) for i in range(n)]
    for copy in copies:
        copy.start()
    for copy in copies:
        copy.wait()


def solution(mesh):
    seq_spec = P('dp', 'tp', None, None)
    head_spec = P('dp', None, 'tp', None)
    col_spec = P(None, None, 'tp')
    ff_spec = P(None, None, None, 'tp')
    peers = mesh.shape['tp']

    def local_step(hidden, lengths, choice, keys_one, vals_one, keys_two, vals_two, g_attn, w_q, w_k, w_v, w_o, g_mlp, w_router, w_gate, w_up, w_down):
        rows, pos, heads, head = keys_one.shape
        dim = hidden.shape[1]
        layers, experts, ff = w_down.shape[:3]
        seq = pos * peers
        flat = lambda t: t.reshape(rows * pos * heads, head)
        turn = lambda t: jnp.swapaxes(t, -1, -2)
        wide = experts * ff
        any_spec = pl.BlockSpec(memory_space=pl.ANY)
        cache_shape = pltpu.VMEM((rows * head, seq), BF16)
        wqkv_rows = w_q.shape[2] + w_k.shape[2] + 2 * w_v.shape[2]
        scratch = [
            pltpu.SMEM((rows,), jnp.int32), pltpu.VMEM((rows, dim), BF16), pltpu.VMEM((layers, choice.shape[2], rows), jnp.int32),
            pltpu.VMEM((layers, dim), BF16), pltpu.VMEM((layers, dim), BF16),
            pltpu.VMEM((4, rows * pos * heads, head), BF16), pltpu.VMEM((4, heads, pos, rows * head), BF16),
            pltpu.VMEM((4, seq, rows * head), BF16),
            pltpu.VMEM((layers, wqkv_rows, dim), BF16), pltpu.VMEM((layers, w_o.shape[1], dim), BF16),
            pltpu.VMEM((layers, experts, dim), BF16),
            pltpu.VMEM((layers, wide, dim), BF16), pltpu.VMEM((layers, wide, dim), BF16), pltpu.VMEM((layers, wide, dim), BF16),
            pltpu.VMEM((LANES, WIDE), BF16), pltpu.VMEM((layers, rows, LANES), F32), pltpu.VMEM((layers, rows, LANES), F32),
            pltpu.VMEM((LANES, seq), F32), pltpu.VMEM((LANES, WIDE), F32),
            pltpu.VMEM((rows, wide), BF16),
            pltpu.VMEM((4, 2, rows, dim // 4), BF16), pltpu.VMEM((4, 2, rows, dim // 4), BF16),
            pltpu.VMEM((4, CHIPS, 2, rows, dim // 4), BF16), pltpu.VMEM((4, 2, 2, rows, dim // 4), BF16),
            pltpu.VMEM((heads, rows * 2, LANES), BF16), pltpu.VMEM((heads, rows * 2, LANES), F32), pltpu.VMEM((heads, rows * 2, LANES), F32),
            pltpu.SemaphoreType.DMA((7,)), pltpu.SemaphoreType.DMA((4,)), pltpu.SemaphoreType.DMA((layers, 3)),
            pltpu.SemaphoreType.DMA((layers,)),
            pltpu.SemaphoreType.DMA((4,)), pltpu.SemaphoreType.DMA((4,)),
            pltpu.SemaphoreType.DMA((4, 2)), pltpu.SemaphoreType.DMA((4, 5)),
            pltpu.SemaphoreType.DMA(()), pltpu.SemaphoreType.DMA(()), pltpu.SemaphoreType.DMA(()), pltpu.SemaphoreType.DMA(()),
        ]
        out = pl.pallas_call(
            kernel,
            name="decode_step",
            out_shape=(pltpu.VMEM((rows, dim), BF16),) + (cache_shape,) * 4,
            in_specs=[any_spec] * 17,
            out_specs=(pl.BlockSpec(memory_space=pltpu.VMEM),) * 5,
            scratch_shapes=scratch,
            compiler_params=pltpu.CompilerParams(collective_id=0, has_side_effects=True, vmem_limit_bytes=64800000),
        )(lengths, hidden, turn(choice), flat(keys_one), flat(vals_one), flat(keys_two), flat(vals_two), g_attn, turn(w_q), turn(w_k), turn(w_v), w_o,
          g_mlp, turn(w_router), turn(w_gate).reshape(layers, wide, dim), turn(w_up).reshape(layers, wide, dim), w_down.reshape(layers, wide, dim))
        out = pl.pallas_call(
            finish,
            name="finish",
            out_shape=[jax.ShapeDtypeStruct(t.shape, t.dtype) for t in out],
            in_specs=[pl.BlockSpec(memory_space=pltpu.VMEM)] * len(out),
            out_specs=[any_spec] * len(out),
            scratch_shapes=[pltpu.SemaphoreType.DMA((len(out),))],
            compiler_params=pltpu.CompilerParams(vmem_limit_bytes=1 << 20),
        )(*[pltpu.with_memory_space_constraint(t, pltpu.VMEM) for t in out])
        caches = [jnp.transpose(t.reshape(rows, head, seq), (0, 2, 1))[:, :, None, :] for t in out[1:]]
        return (out[0], *caches)

    return jax.shard_map(local_step, mesh=mesh, in_specs=(P('dp', None), P('dp'), P(None, 'dp', None), seq_spec, seq_spec, seq_spec, seq_spec, P(), col_spec, col_spec, col_spec, P(None, 'tp', None), P(), P(), ff_spec, ff_spec, P(None, None, 'tp', None)), out_specs=(P('dp', None), head_spec, head_spec, head_spec, head_spec), check_vma=False)
```

time: 65.5 us -> 58.5 us (0.89)
  Pallas kernels: 64.6 us -> 57.6 us
    pallas_call x1, Pallas kernels: 62.1 us -> 56.2 us  [local_step(): pl.pallas_call(kernel, name='decode_step', out_shape=(pltpu.VMEM((rows, d...]
    pallas_call x1, Pallas kernels: 2.5 us -> 1.39 us  [local_step(): pl.pallas_call(finish, name='finish', out_shape=[jax.ShapeDtypeStruct(t.s...]
where the time goes in v3:
time: 58.5 us; the launch traced here: 58.4 us
  Pallas kernels  57.6 us (98%)
  between operations  0.81 us (1%)
    pallas_call x1, Pallas kernels, local_step(): pl.pallas_call(kernel, name='decode_step', out_shape=(pltpu.VMEM((rows, d...  56.2 us
    pallas_call x1, Pallas kernels, local_step(): pl.pallas_call(finish, name='finish', out_shape=[jax.ShapeDtypeStruct(t.s...  1.39 us

profile of v3, /device:TPU:113, one launch (start us, length us, event | category | flops | bytes accessed | tf_op | source)
XLA Modules:
  0.0 58.4 jit_solution(8498764051171346251)
XLA Ops:
  0.6 56.2 %decode_step.1 = (bf16[32,1536]{1,0:T(8,128)(2,1)S(1)}, bf16[2048,128]{1,0:T(8,128)(2,1)S(1)}, bf16[2048,128]{1,0:T(8,128)(2,1)S(1)}, bf16[2048,128]{1,0:T(8,128)(2,1)S(1)}, bf16[2048,128]{1,0:T(8,128)(2,1)S(1)}) custom-call(s32[32]{0:T(128)} %len_h.1, bf16[32,1536]{1,0:T(8,128)(2,1)} %hid_h.1, s32[2,8,32]{2,1,0:T(8,128)} %bitcast.47, ...), custom_call_target="tpu_custom_call" | custom-call | tf_op jit(solution)/shard_map/decode_step/pallas_call | solution.py:541
  56.9 1.4 %finish.1 = (bf16[32,1536]{1,0:T(8,128)(2,1)}, bf16[2048,128]{1,0:T(8,128)(2,1)}, bf16[2048,128]{1,0:T(8,128)(2,1)}, bf16[2048,128]{1,0:T(8,128)(2,1)}, bf16[2048,128]{1,0:T(8,128)(2,1)}) custom-call(bf16[32,1536]{1,0:T(8,128)(2,1)S(1)} %get-tuple-element.15.refs_0_, bf16[2048,128]{1,0:T(8,128)(2,1)S(1)} %get-tuple-element.16.refs_1_, ...), custom_call_target="tpu_custom_call" | custom-call | tf_op jit(solution)/shard_map/finish/pallas_call | solution.py:551

commit v4 on v3

--- a/solution.py
+++ b/solution.py
@@ -21,13 +21,13 @@
 
 
 WINDOWS = (
+    units(1, 0, 1, 2, 3, 4),
+    [],
+    units(3, 4) + units(2, 4, 0, 1),
     units(2, 2),
-    units(2, 4, 0) + units(3, 4),
-    [],
-    units(2, 1),
     units(2, 3) + units(3, 0, 1, 2, 3),
-    units(0, 4, 0, 1, 2) + units(1, 4),
-    units(0, 3) + units(1, 0, 1, 2, 3),
+    units(0, 4, 0, 1),
+    units(0, 2, 3),
 )
 CHUNKS = 10
 
@@ -89,7 +89,7 @@
     barrier = pltpu.get_barrier_semaphore()
     for dx, flip in OFFSETS:
         pl.semaphore_signal(barrier, inc=1, device_id={"tp": device(dx, flip)}, device_id_type=MESH)
-    for c in (2, 0, 1, 3):
+    for c in (1, 0, 2, 3):
         loads[c].start()
     for copy in small[4:]:
         copy.start()
@@ -163,11 +163,11 @@
     def block_queries(q3):
         i, j = iota((LANES, 96), 0), iota((LANES, 96), 1)
         slot = lax.rem(i, TILE)
-        pick = (slot < 12) & (j == lax.rem(slot, 3) * rows + i // TILE * 4 + slot // 3)
+        pick = (lax.rem(slot, 4) < 3) & (j == lax.rem(slot, 4) * rows + i // 4)
         dup = nn(pick.astype(BF16), q3)
         slot2, lane2 = lax.rem(iota((LANES, WIDE), 0), TILE), iota((LANES, WIDE), 1)
         both = jnp.concatenate([dup, dup], axis=1)
-        qall[...] = jnp.where(slot2 // 3 == lane2 // HEAD, both, 0.0).astype(BF16)
+        qall[...] = jnp.where(slot2 // 4 == lane2 // HEAD, both, 0.0).astype(BF16)
 
     hb = rows // 2
     prow, plane = iota((hb * 4, LANES), 0), iota((hb * 4, LANES), 1)
@@ -198,72 +198,50 @@
     def seven(ref):
         return ref.at[pl.ds(0, len(OFFSETS))]
 
-    def local_attend():
-        row_i, lane_i = iota((LANES, LANES), 0), iota((LANES, LANES), 1)
+    def local_scores():
         wide_row, wide_lane = iota((LANES, WIDE), 0), iota((LANES, WIDE), 1)
-        own_head = row_i // TILE == lax.rem(lane_i, 8)
-        where_pos = me * pos + lane_i // 8
-        in_group = lax.rem(row_i, TILE) // 4
-        slot = lax.rem(row_i, 4)
         diagonal = wide_lane // head == lax.rem(wide_row, TILE) // 4
-        half_lane = lane_i < head
-        lane_in = lax.rem(lane_i, head)
-        done = []
+        half_lane = iota((LANES, LANES), 1) < head
+        lane_block = iota((TILE, LANES), 1) // pos
+        kept = [jnp.zeros((TILE, LANES), F32)] * 8
         for t in range(groups):
             at = slice(t % 4 * TILE, t % 4 * TILE + TILE)
             q = qrecv[:, at, :].reshape(LANES, LANES).astype(F32)
             q = jnp.where(half_lane if t < 4 else ~half_lane, q, 0.0)
             q = q + pltpu.roll(q, HEAD, 1)
             q = jnp.where(diagonal, jnp.concatenate([q, q], axis=1), 0.0).astype(BF16)
-            keys = jnp.concatenate([xst[0, b * LANES:(b + 1) * LANES, :] for b in range(4 * t, 4 * t + 4)], axis=1)
-            vals = jnp.concatenate([xst[1, b * LANES:(b + 1) * LANES, :] for b in range(4 * t, 4 * t + 4)], axis=1)
+            keys = sendb[0, :, :, t * WIDE:(t + 1) * WIDE].reshape(LANES, WIDE)
             s = nt(q, keys) * (head ** -0.5)
-            limit = jnp.where(in_group == 0, len_s[4 * t], jnp.where(in_group == 1, len_s[4 * t + 1], jnp.where(in_group == 2, len_s[4 * t + 2], len_s[4 * t + 3])))
-            valid = own_head & (where_pos < limit)
-            s = jnp.where(valid, s, -1e30)
-            top = jnp.max(s, axis=-1, keepdims=True)
-            p = jnp.where(valid, jnp.exp(s - top), 0.0)
-            total = jnp.sum(p, axis=-1, keepdims=True)
-            o = jnp.where(diagonal, nn(p.astype(BF16), vals), 0.0)
-            o = o[:, :LANES] + o[:, LANES:]
-            o = o + pltpu.roll(o, HEAD, 1)
-            stat = jnp.where(slot == 3, 0.0, jnp.where(lane_in == slot, top, jnp.where(lane_in == slot + 3, total, 0.0)))
-            stat = pltpu.roll(stat, 1, 0) + pltpu.roll(stat, 2, 0) + pltpu.roll(stat, 3, 0)
-            done.append(jnp.where(slot == 3, stat, o))
-            if t >= 4:
-                psend[:, at, :] = jnp.where(half_lane, done[t - 4], done[t]).reshape(8, TILE, LANES)
+            for h in range(8):
+                turned = s[h * TILE:(h + 1) * TILE, :]
+                if h != t:
+                    turned = pltpu.roll(turned, (t - h) % 8 * pos, 1)
+                kept[h] = jnp.where(lane_block == t, turned, kept[h])
+        for h in range(8):
+            psend[h] = kept[h]
 
     def half_sum(x):
         low_half = jnp.sum(jnp.where(pleft, x, 0.0), axis=-1, keepdims=True)
         high_half = jnp.sum(jnp.where(pleft, 0.0, x), axis=-1, keepdims=True)
         return jnp.where(pleft, low_half, high_half)
 
-    def merge(queries, fresh_k, fresh_v):
-        slot, lane_in = lax.rem(prow, 4), lax.rem(plane, head)
-        n_rows = prow.shape[0]
-        parts = []
-        for n in range(2 * CHIPS):
-            x = precv[n]
-            stat = jnp.where(slot == 0, pltpu.roll(x, n_rows - 3, 0), jnp.where(slot == 1, pltpu.roll(x, n_rows - 2, 0), pltpu.roll(x, n_rows - 1, 0)))
-            parts.append((half_sum(jnp.where(lane_in == slot, stat, 0.0)), half_sum(jnp.where(lane_in == slot + 3, stat, 0.0)), x))
-        own = half_sum(queries * fresh_k) * (head ** -0.5)
-        top = own
-        for m, _, _ in parts:
-            top = jnp.maximum(top, m)
-        weight = jnp.exp(own - top)
-        den, num = weight, weight * fresh_v
-        for m, total, o in parts:
-            weight = jnp.exp(m - top)
-            den += weight * total
-            num += weight * o
-        o = jnp.where(slot == 3, 0.0, num / den).astype(BF16)
-        i, j = iota((rows, n_rows), 0), iota((rows, n_rows), 1)
-        kept = left == (row < hb)
-        per_head = []
-        for r in range(3):
-            got = jnp.where(kept, nn((j == lax.rem(i, hb) * 4 + r).astype(BF16), o), 0.0)
-            per_head.append(got + pltpu.roll(got, HEAD, 1))
-        return jnp.where(left, per_head[0], per_head[1]).astype(BF16), per_head[2].astype(BF16)[:, :head]
+    def gathered_scores(own):
+        lane_block = iota((TILE, LANES), 1) // pos
+        for t in range(groups):
+            tile = precv[t]
+            for j in range(2 * CHIPS):
+                turned = precv[j]
+                if j != t:
+                    turned = pltpu.roll(turned, (j - t) % 8 * pos, 1)
+                tile = jnp.where(lane_block == j, turned, tile)
+            sc[t * TILE:(t + 1) * TILE, :] = tile
+        fresh = jnp.concatenate([own[:, :1], own[:, head:head + 1]], axis=0)
+        limit = jnp.zeros((LANES, LANES), jnp.int32)
+        row_i, lane_i = iota((LANES, LANES), 0) // 4, iota((LANES, LANES), 1)
+        for b in range(rows):
+            limit = jnp.where(row_i == b, len_s[b], limit)
+        s = jnp.where(lane_i == limit, fresh, sc[...])
+        return jnp.where(lane_i <= limit, s, -1e30)
 
     def place_new(c, t, fresh, layer):
         at = slice(t * WIDE, t * WIDE + WIDE)
@@ -279,8 +257,8 @@
         recvb[c, :, at] = tile
         return tile
 
-    def attend(layer):
-        ck, cv = 2 * layer, 2 * layer + 1
+    def layer_scores(layer):
+        ck = 2 * layer
         with jax.named_scope("wait_keys"):
             a2a_wait(ck)
 
@@ -288,13 +266,16 @@
             tile = place_new(ck, t, kdup, layer)
             at = slice(t * TILE, t * TILE + TILE)
             s = nt(qall[at, :], tile) * (head ** -0.5)
-            slot, p = iota((TILE, seq), 0), iota((TILE, seq), 1)
-            limit = jnp.where(slot < 3, len_s[4 * t], jnp.where(slot < 6, len_s[4 * t + 1], jnp.where(slot < 9, len_s[4 * t + 2], len_s[4 * t + 3])))
+            slot, p = iota((TILE, seq), 0) // 4, iota((TILE, seq), 1)
+            limit = jnp.where(slot == 0, len_s[4 * t], jnp.where(slot == 1, len_s[4 * t + 1], jnp.where(slot == 2, len_s[4 * t + 2], len_s[4 * t + 3])))
             sc[at, :] = jnp.where(p <= limit, s, -1e30)
         with jax.named_scope("scores"):
             for t in range(groups):
                 scores(t)
-        s = sc[...]
+        return sc[...]
+
+    def attend(layer, s):
+        cv = 2 * layer + 1
         e = jnp.exp(s - jnp.max(s, axis=-1, keepdims=True))
         sc[...] = e / jnp.sum(e, axis=-1, keepdims=True)
         with jax.named_scope("wait_values"):
@@ -308,13 +289,12 @@
             for t in range(groups):
                 values(t)
         slot2, lane2 = lax.rem(iota((LANES, WIDE), 0), TILE), iota((LANES, WIDE), 1)
-        kept = jnp.where(slot2 // 3 == lane2 // HEAD, ov[...], 0.0)
+        kept = jnp.where(slot2 // 4 == lane2 // HEAD, ov[...], 0.0)
         both = (kept[:, :LANES] + kept[:, LANES:]).astype(BF16)
         i, j = iota((rows, LANES), 0), iota((rows, LANES), 1)
         per_head = []
         for r in range(3):
-            pick = j == i // 4 * TILE + lax.rem(i, 4) * 3 + r
-            got = nn(pick.astype(BF16), both)
+            got = nn((j == i * 4 + r).astype(BF16), both)
             per_head.append(got + pltpu.roll(got, HEAD, 1))
         return jnp.where(left, per_head[0], per_head[1]).astype(BF16), per_head[2].astype(BF16)[:, :head]
 
@@ -391,7 +371,7 @@
         for c in range(CHUNKS):
             at = slice(c * step, (c + 1) * step)
             g = nt(m, wg[layer, at, :])
-            up = nt(m, wu[layer, at, :])
+            up = nt(wu[layer, at, :], m).T
             wide = jnp.concatenate([jnp.where(left, gate[:, 2 * n:2 * n + 1], gate[:, 2 * n + 1:2 * n + 2]) for n in range(c * pairs, (c + 1) * pairs)], axis=1)
             ubuf[:, at] = (jax.nn.silu(g) * up * wide).astype(BF16)
 
@@ -403,20 +383,24 @@
     with jax.named_scope("project"):
         q3 = project(0, x)
         queries = pack_queries(q3)
-        fresh_k, fresh_v = pack_fresh(kdup[0]), pack_fresh(vdup[0])
         qrecv[me] = queries.astype(BF16)
     with jax.named_scope("barrier"):
         pl.semaphore_wait(barrier, len(OFFSETS))
     for n in range(7):
         q_copy(n).start()
-    with jax.named_scope("permute2"):
-        loads[2].wait()
-        permute(2)
+    with jax.named_scope("permute1"):
+        loads[1].wait()
+        permute(1)
+    with jax.named_scope("permute_rest"):
+        loads[0].wait()
+        permute(0)
     send_caches(WINDOWS[0])
-    with jax.named_scope("permute_rest"):
+    with jax.named_scope("own_score"):
+        own_score = half_sum(queries * pack_fresh(kdup[0])) * (head ** -0.5)
+    with jax.named_scope("permute23"):
         for copy in small[4:]:
             copy.wait()
-        for c in (3, 0, 1):
+        for c in (2, 3):
             loads[c].wait()
             permute(c)
         for c in range(4):
@@ -424,23 +408,24 @@
     with jax.named_scope("q_wait"):
         drain(seven(qrecv), rs_q)
     send_caches(WINDOWS[1])
-    with jax.named_scope("local_attend"):
-        local_attend()
+    with jax.named_scope("local_scores"):
+        local_scores()
     for n in range(7):
         p_copy(n).start()
+    send_caches(WINDOWS[2])
     precv[me] = psend[me]
-    send_caches(WINDOWS[2])
     with jax.named_scope("p_wait"):
         drain(seven(precv), rs_p)
     send_caches(WINDOWS[3])
     with jax.named_scope("merge"):
-        first, second = merge(queries, fresh_k, fresh_v)
+        s = gathered_scores(own_score)
 
     for layer in range(2):
         if layer:
             with jax.named_scope("project"):
                 block_queries(project(layer, x))
-            first, second = attend(layer)
+            s = layer_scores(layer)
+        first, second = attend(layer, s)
         n1 = first.shape[1]
 
         def out_product(which, q, size, layer=layer, first=first, second=second, n1=n1):
@@ -451,15 +436,16 @@
             if layer:
                 write_out(2)
                 write_out(3)
+            else:
+                write_out(1)
             wait_weights(layer)
 
         def between_moe(layer=layer):
             if layer:
-                for c, fresh in ((0, kdup), (1, vdup)):
-                    a2a_wait(c)
-                    for t in range(groups):
-                        place_new(c, t, fresh, 0)
-                    write_out(c)
+                a2a_wait(0)
+                for t in range(groups):
+                    place_new(0, t, kdup, 0)
+                write_out(0)
 
         def residual_attn(q, size, layer=layer):
             if layer:
@@ -531,7 +517,7 @@
             pltpu.VMEM((rows, wide), BF16),
             pltpu.VMEM((4, 2, rows, dim // 4), BF16), pltpu.VMEM((4, 2, rows, dim // 4), BF16),
             pltpu.VMEM((4, CHIPS, 2, rows, dim // 4), BF16), pltpu.VMEM((4, 2, 2, rows, dim // 4), BF16),
-            pltpu.VMEM((heads, rows * 2, LANES), BF16), pltpu.VMEM((heads, rows * 2, LANES), F32), pltpu.VMEM((heads, rows * 2, LANES), F32),
+            pltpu.VMEM((heads, rows * 2, LANES), BF16), pltpu.VMEM((heads, TILE, LANES), F32), pltpu.VMEM((heads, TILE, LANES), F32),
             pltpu.SemaphoreType.DMA((7,)), pltpu.SemaphoreType.DMA((4,)), pltpu.SemaphoreType.DMA((layers, 3)),
             pltpu.SemaphoreType.DMA((layers,)),
             pltpu.SemaphoreType.DMA((4,)), pltpu.SemaphoreType.DMA((4,)),

time: 58.5 us -> 57.3 us (0.979)
  Pallas kernels: 57.6 us -> 56.6 us
    pallas_call x1, Pallas kernels: 56.2 us -> 55.2 us  [local_step(): pl.pallas_call(kernel, name='decode_step', out_shape=(pltpu.VMEM((rows, d...]
where the time goes in v4:
time: 57.3 us
  Pallas kernels  56.6 us (99%)
  between operations  0.65 us (1%)
    pallas_call x1, Pallas kernels, local_step(): pl.pallas_call(kernel, name='decode_step', out_shape=(pltpu.VMEM((rows, d...  55.2 us
    pallas_call x1, Pallas kernels, local_step(): pl.pallas_call(finish, name='finish', out_shape=[jax.ShapeDtypeStruct(t.s...  1.39 us

profile of v4, /device:TPU:113, one launch (start us, length us, event | category | flops | bytes accessed | tf_op | source)
XLA Modules:
  0.0 57.3 jit_solution(11517025443496109177)
XLA Ops:
  0.6 55.2 %decode_step.1 = (bf16[32,1536]{1,0:T(8,128)(2,1)S(1)}, bf16[2048,128]{1,0:T(8,128)(2,1)S(1)}, bf16[2048,128]{1,0:T(8,128)(2,1)S(1)}, bf16[2048,128]{1,0:T(8,128)(2,1)S(1)}, bf16[2048,128]{1,0:T(8,128)(2,1)S(1)}) custom-call(s32[32]{0:T(128)} %len_h.1, bf16[32,1536]{1,0:T(8,128)(2,1)} %hid_h.1, s32[2,8,32]{2,1,0:T(8,128)} %bitcast.47, ...), custom_call_target="tpu_custom_call" | custom-call | tf_op jit(solution)/shard_map/decode_step/pallas_call | solution.py:527
  55.9 1.4 %finish.1 = (bf16[32,1536]{1,0:T(8,128)(2,1)}, bf16[2048,128]{1,0:T(8,128)(2,1)}, bf16[2048,128]{1,0:T(8,128)(2,1)}, bf16[2048,128]{1,0:T(8,128)(2,1)}, bf16[2048,128]{1,0:T(8,128)(2,1)}) custom-call(bf16[32,1536]{1,0:T(8,128)(2,1)S(1)} %get-tuple-element.15.refs_0_, bf16[2048,128]{1,0:T(8,128)(2,1)S(1)} %get-tuple-element.16.refs_1_, ...), custom_call_target="tpu_custom_call" | custom-call | tf_op jit(solution)/shard_map/finish/pallas_call | solution.py:537

commit v5 on v4

--- a/solution.py
+++ b/solution.py
@@ -21,7 +21,7 @@
 
 
 WINDOWS = (
-    units(1, 0, 1, 2, 3, 4),
+    units(1, 2, 3, 0, 1, 4),
     [],
     units(3, 4) + units(2, 4, 0, 1),
     units(2, 2),
@@ -47,7 +47,7 @@
 def kernel(len_h, hid_h, choice_h, k1_h, v1_h, k2_h, v2_h, ga_h, wq_h, wk_h, wv_h, wo_h, gm_h, wr_h, wg_h, wu_h, wd_h,
            out_hid, ok1, ov1, ok2, ov2,
            len_s, hid, choice, ga, gm, xst, sendb, recvb, wqkv, wo, wr, wg, wu, wd,
-           qall, kdup, vdup, sc, ov, ubuf, part, d1, shot, fin, qrecv, psend, precv,
+           qall, kdup, vdup, turns, sc, ov, ubuf, part, d1, shot, fin, qrecv, psend, precv,
            sem_small, sem_x, sem_w, sem_wqkv, ss_a, rs_a, ss_r, rs_r, ss_q, rs_q, ss_p, rs_p):
     rows, dim = hid.shape
     half = dim // 2
@@ -74,17 +74,18 @@
 
     loads = [pltpu.make_async_copy(src, xst.at[c], sem_x.at[c]) for c, src in enumerate((k1_h, v1_h, k2_h, v2_h))]
     small = [pltpu.make_async_copy(src, dst, sem_small.at[n]) for n, (src, dst) in enumerate(
-        ((hid_h, hid), (len_h, len_s), (ga_h, ga), (gm_h, gm), (choice_h, choice), (wr_h, wr), (wo_h, wo)))]
+        ((len_h, len_s), (hid_h, hid), (ga_h, ga), (gm_h, gm), (choice_h, choice), (wr_h, wr), (wo_h, wo)))]
 
     def qkv_loads(layer):
         nq, nk = wq_h.shape[1], wk_h.shape[1]
         return [pltpu.make_async_copy(src.at[layer], wqkv.at[layer, pl.ds(at, size)], sem_wqkv.at[layer])
                 for src, at, size in ((wq_h, 0, nq), (wk_h, nq, nk), (wv_h, nq + nk, nk), (wv_h, nq + 2 * nk, nk))]
 
-    small[0].start()
+    for copy in small[:2]:
+        copy.start()
     for copy in qkv_loads(0):
         copy.start()
-    for copy in small[1:4]:
+    for copy in small[2:4]:
         copy.start()
     barrier = pltpu.get_barrier_semaphore()
     for dx, flip in OFFSETS:
@@ -128,9 +129,8 @@
             return 0
         lax.fori_loop(0, CHUNKS, start_weights, 0)
 
-    with jax.named_scope("small_wait"):
-        for copy in small[:4]:
-            copy.wait()
+    with jax.named_scope("len_wait"):
+        small[0].wait()
     lane = iota((rows, LANES), 1)
     row = iota((rows, LANES), 0)
     len_f = jnp.zeros((rows, LANES), F32)
@@ -138,13 +138,13 @@
         len_f = jnp.where(row == b, len_s[b].astype(F32), len_f)
     freq = jnp.exp(lax.rem(lane, 32).astype(F32) * (-2.0 / head * 13.815510557964274))
     angle = len_f * freq
-    cos_t, sin_t = jnp.cos(angle), jnp.sin(angle)
+    turns[0], turns[1] = jnp.cos(angle), jnp.sin(angle)
     low = lax.rem(lane, head) < head // 2
     left = lane < head
 
     def rope(x):
         turned = jnp.where(low, -pltpu.roll(x, 96, 1), pltpu.roll(x, 32, 1))
-        return (x * cos_t + turned * sin_t).astype(BF16).astype(F32)
+        return (x * turns[0] + turned * turns[1]).astype(BF16).astype(F32)
 
     def norm(x, gain):
         scale = lax.rsqrt(jnp.mean(x * x, axis=-1, keepdims=True) + EPS)
@@ -304,47 +304,42 @@
         for t in range(groups):
             outs[c][t * WIDE:(t + 1) * WIDE, :] = recvb[c, :, t * WIDE:(t + 1) * WIDE].T
 
-    def cols(which):
-        return pl.ds(pl.multiple_of(which * half, half), half)
-
-    def block(which, q, size):
-        return pl.ds(pl.multiple_of(which * half + q * size, size), size)
+    unit = shot.shape[4]
+
+    def block(which, at, n):
+        return pl.ds(pl.multiple_of(which * half + at * unit, unit), n * unit)
+
+    def put(ref, at, n, value):
+        for k in range(n):
+            ref[at + k] = value[:, k * unit:(k + 1) * unit].astype(BF16)
+
+    def get(ref, at, n):
+        return jnp.concatenate([ref[at + k].astype(F32) for k in range(n)], axis=1)
 
     def all_reduce(r, product, residual, between, parts, window):
-        size = half // parts
-        per = shot.shape[2] // parts
-
         def send(ref, dst, ssem, rsem, peer):
             rcopy(ref, dst, ss_r.at[r, ssem], rs_r.at[r, rsem], peer).start()
 
-        def put(ref, q, value):
-            for n in range(per):
-                ref[q * per + n] = value[:, n * (size // per):(n + 1) * (size // per)].astype(BF16)
-
-        def get(ref, q):
-            return jnp.concatenate([ref[q * per + n].astype(F32) for n in range(per)], axis=1)
-
-        for q in range(parts):
-            put(part.at[r], q, product(1 - core, q, size))
-            at = pl.ds(q * per, per)
-            send(part.at[r, at], d1.at[r, at], 0, q, partner)
-        for q in range(parts):
-            mine = product(core, q, size)
+        for q, (at, n) in enumerate(parts):
+            put(part.at[r], at, n, product(1 - core, at, n))
+            send(part.at[r, pl.ds(at, n)], d1.at[r, pl.ds(at, n)], 0, q, partner)
+        for q, (at, n) in enumerate(parts):
+            mine = product(core, at, n)
             with jax.named_scope("swap_wait"):
-                drain(d1.at[r, pl.ds(q * per, per)], rs_r.at[r, q])
-            put(shot.at[r, chip], q, mine + get(d1.at[r], q))
-            piece = shot.at[r, chip, pl.ds(q * per, per)]
+                drain(d1.at[r, pl.ds(at, n)], rs_r.at[r, q])
+            put(shot.at[r, chip], at, n, mine + get(d1.at[r], at, n))
+            piece = shot.at[r, chip, pl.ds(at, n)]
             for dx in (2, 1, 3):
                 send(piece, piece, 1, 2 + q, device(dx, 0))
         with jax.named_scope("between"):
             between()
-        for q in range(parts):
-            at = pl.ds(q * per, per)
+        for q, (at, n) in enumerate(parts):
             with jax.named_scope("shot_wait"):
-                drain(shot.at[r, pl.ds(0, CHIPS - 1), at], rs_r.at[r, 2 + q])
-            total = (get(shot.at[r, 0], q) + get(shot.at[r, 1], q)) + (get(shot.at[r, 2], q) + get(shot.at[r, 3], q))
-            put(fin.at[r, core], q, residual(q, size) + total)
-            send(fin.at[r, core, at], fin.at[r, core, at], 0, 4, partner)
+                drain(shot.at[r, pl.ds(0, CHIPS - 1), pl.ds(at, n)], rs_r.at[r, 2 + q])
+            total = (get(shot.at[r, 0], at, n) + get(shot.at[r, 1], at, n)) + (get(shot.at[r, 2], at, n) + get(shot.at[r, 3], at, n))
+            put(fin.at[r, core], at, n, residual(at, n) + total)
+            piece = fin.at[r, core, pl.ds(at, n)]
+            send(piece, piece, 0, 4, partner)
         send_caches(window)
         with jax.named_scope("last_wait"):
             drain(fin.at[r, 1 - core], rs_r.at[r, 4])
@@ -379,6 +374,9 @@
         for c, n in wanted:
             a2a_copy(c, n).start()
 
+    with jax.named_scope("small_wait"):
+        for copy in small[1:4]:
+            copy.wait()
     x = hid[...].astype(F32)
     with jax.named_scope("project"):
         q3 = project(0, x)
@@ -428,9 +426,9 @@
         first, second = attend(layer, s)
         n1 = first.shape[1]
 
-        def out_product(which, q, size, layer=layer, first=first, second=second, n1=n1):
-            at = block(which, q, size)
-            return nn(first, wo[layer, :n1, at]) + nn(second, wo[layer, n1:, at])
+        def out_product(which, at, n, layer=layer, first=first, second=second, n1=n1):
+            cols = block(which, at, n)
+            return nn(first, wo[layer, :n1, cols]) + nn(second, wo[layer, n1:, cols])
 
         def between_attn(layer=layer):
             if layer:
@@ -447,24 +445,22 @@
                     place_new(0, t, kdup, 0)
                 write_out(0)
 
-        def residual_attn(q, size, layer=layer):
-            if layer:
-                return jnp.concatenate([fin[2 * layer - 1, core, n].astype(F32) for n in range(shot.shape[2])], axis=1)
-            return hid[:, block(core, q, size)].astype(F32)
-
-        x = all_reduce(2 * layer, out_product, residual_attn, between_attn, 1, WINDOWS[4 + 2 * layer])
+        def residual_attn(at, n, layer=layer):
+            return get(fin.at[2 * layer - 1, core], at, n) if layer else hid[:, block(core, at, n)].astype(F32)
+
+        x = all_reduce(2 * layer, out_product, residual_attn, between_attn, ((0, 3),), WINDOWS[4 + 2 * layer])
         m = norm(x, gm[layer:layer + 1, :])
         with jax.named_scope("up"):
             experts_up(layer, m)
 
-        def down_product(which, q, size, layer=layer):
+        def down_product(which, at, n, layer=layer):
             with jax.named_scope("down"):
-                return nn(ubuf[...], wd[layer, :, block(which, q, size)])
-
-        def residual_moe(q, size, layer=layer):
-            return fin[2 * layer, core, q].astype(F32)
-
-        x = all_reduce(2 * layer + 1, down_product, residual_moe, between_moe, 2, () if layer else WINDOWS[5])
+                return nn(ubuf[...], wd[layer, :, block(which, at, n)])
+
+        def residual_moe(at, n, layer=layer):
+            return get(fin.at[2 * layer, core], at, n)
+
+        x = all_reduce(2 * layer + 1, down_product, residual_moe, between_moe, ((0, 2), (2, 1)), () if layer else WINDOWS[5])
     out_hid[...] = x.astype(BF16)
 
     with jax.named_scope("tail"):
@@ -512,11 +508,11 @@
             pltpu.VMEM((layers, wqkv_rows, dim), BF16), pltpu.VMEM((layers, w_o.shape[1], dim), BF16),
             pltpu.VMEM((layers, experts, dim), BF16),
             pltpu.VMEM((layers, wide, dim), BF16), pltpu.VMEM((layers, wide, dim), BF16), pltpu.VMEM((layers, wide, dim), BF16),
-            pltpu.VMEM((LANES, WIDE), BF16), pltpu.VMEM((layers, rows, LANES), F32), pltpu.VMEM((layers, rows, LANES), F32),
+            pltpu.VMEM((LANES, WIDE), BF16), pltpu.VMEM((layers, rows, LANES), F32), pltpu.VMEM((layers, rows, LANES), F32), pltpu.VMEM((2, rows, LANES), F32),
             pltpu.VMEM((LANES, seq), F32), pltpu.VMEM((LANES, WIDE), F32),
             pltpu.VMEM((rows, wide), BF16),
-            pltpu.VMEM((4, 2, rows, dim // 4), BF16), pltpu.VMEM((4, 2, rows, dim // 4), BF16),
-            pltpu.VMEM((4, CHIPS, 2, rows, dim // 4), BF16), pltpu.VMEM((4, 2, 2, rows, dim // 4), BF16),
+            pltpu.VMEM((4, 3, rows, dim // 6), BF16), pltpu.VMEM((4, 3, rows, dim // 6), BF16),
+            pltpu.VMEM((4, CHIPS, 3, rows, dim // 6), BF16), pltpu.VMEM((4, 2, 3, rows, dim // 6), BF16),
             pltpu.VMEM((heads, rows * 2, LANES), BF16), pltpu.VMEM((heads, TILE, LANES), F32), pltpu.VMEM((heads, TILE, LANES), F32),
             pltpu.SemaphoreType.DMA((7,)), pltpu.SemaphoreType.DMA((4,)), pltpu.SemaphoreType.DMA((layers, 3)),
             pltpu.SemaphoreType.DMA((layers,)),

time: 57.3 us -> 57 us (level)
  no operation moved by 1% of the time
where the time goes in v5:
time: 57 us; the launch traced here: 56.9 us
  Pallas kernels  56.3 us (99%)
  between operations  0.65 us (1%)
    pallas_call x1, Pallas kernels, local_step(): pl.pallas_call(kernel, name='decode_step', out_shape=(pltpu.VMEM((rows, d...  54.9 us
    pallas_call x1, Pallas kernels, local_step(): pl.pallas_call(finish, name='finish', out_shape=[jax.ShapeDtypeStruct(t.s...  1.39 us

profile of v5, /device:TPU:113, one launch (start us, length us, event | category | flops | bytes accessed | tf_op | source)
XLA Modules:
  0.0 56.9 jit_solution(12429858995652118773)
XLA Ops:
  0.6 54.9 %decode_step.1 = (bf16[32,1536]{1,0:T(8,128)(2,1)S(1)}, bf16[2048,128]{1,0:T(8,128)(2,1)S(1)}, bf16[2048,128]{1,0:T(8,128)(2,1)S(1)}, bf16[2048,128]{1,0:T(8,128)(2,1)S(1)}, bf16[2048,128]{1,0:T(8,128)(2,1)S(1)}) custom-call(s32[32]{0:T(128)} %len_h.1, bf16[32,1536]{1,0:T(8,128)(2,1)} %hid_h.1, s32[2,8,32]{2,1,0:T(8,128)} %bitcast.47, ...), custom_call_target="tpu_custom_call" | custom-call | tf_op jit(solution)/shard_map/decode_step/pallas_call | solution.py:523
  55.5 1.4 %finish.1 = (bf16[32,1536]{1,0:T(8,128)(2,1)}, bf16[2048,128]{1,0:T(8,128)(2,1)}, bf16[2048,128]{1,0:T(8,128)(2,1)}, bf16[2048,128]{1,0:T(8,128)(2,1)}, bf16[2048,128]{1,0:T(8,128)(2,1)}) custom-call(bf16[32,1536]{1,0:T(8,128)(2,1)S(1)} %get-tuple-element.15.refs_0_, bf16[2048,128]{1,0:T(8,128)(2,1)S(1)} %get-tuple-element.16.refs_1_, ...), custom_call_target="tpu_custom_call" | custom-call | tf_op jit(solution)/shard_map/finish/pallas_call | solution.py:533

commit v6 on v5

--- a/solution.py
+++ b/solution.py
@@ -318,7 +318,7 @@
 
     def all_reduce(r, product, residual, between, parts, window):
         def send(ref, dst, ssem, rsem, peer):
-            rcopy(ref, dst, ss_r.at[r, ssem], rs_r.at[r, rsem], peer).start()
+            rcopy(ref, dst, ss_r.at[ssem], rs_r.at[r, rsem], peer).start()
 
         for q, (at, n) in enumerate(parts):
             put(part.at[r], at, n, product(1 - core, at, n))
@@ -464,9 +464,8 @@
     out_hid[...] = x.astype(BF16)
 
     with jax.named_scope("tail"):
-        for r in range(4):
-            drain(shot.at[r, pl.ds(0, 2)], ss_r.at[r, 0])
-            drain(shot.at[r, pl.ds(0, CHIPS - 1)], ss_r.at[r, 1])
+        drain(shot.at[:, pl.ds(0, 2)], ss_r.at[0])
+        drain(shot.at[:, pl.ds(0, CHIPS - 1)], ss_r.at[1])
         drain(seven(qrecv), ss_q)
         drain(seven(psend), ss_p)
         for c in range(4):
@@ -517,7 +516,7 @@
             pltpu.SemaphoreType.DMA((7,)), pltpu.SemaphoreType.DMA((4,)), pltpu.SemaphoreType.DMA((layers, 3)),
             pltpu.SemaphoreType.DMA((layers,)),
             pltpu.SemaphoreType.DMA((4,)), pltpu.SemaphoreType.DMA((4,)),
-            pltpu.SemaphoreType.DMA((4, 2)), pltpu.SemaphoreType.DMA((4, 5)),
+            pltpu.SemaphoreType.DMA((2,)), pltpu.SemaphoreType.DMA((4, 5)),
             pltpu.SemaphoreType.DMA(()), pltpu.SemaphoreType.DMA(()), pltpu.SemaphoreType.DMA(()), pltpu.SemaphoreType.DMA(()),
         ]
         out = pl.pallas_call(

time: 57 us -> 56.9 us (level)
  no operation moved by 1% of the time
where the time goes in v6:
time: 56.9 us
  Pallas kernels  56.2 us (99%)
  between operations  0.65 us (1%)
    pallas_call x1, Pallas kernels, local_step(): pl.pallas_call(kernel, name='decode_step', out_shape=(pltpu.VMEM((rows, d...  54.8 us
    pallas_call x1, Pallas kernels, local_step(): pl.pallas_call(finish, name='finish', out_shape=[jax.ShapeDtypeStruct(t.s...  1.39 us

profile of v6, /device:TPU:113, one launch (start us, length us, event | category | flops | bytes accessed | tf_op | source)
XLA Modules:
  0.0 56.9 jit_solution(4780015271657636611)
XLA Ops:
  0.6 54.8 %decode_step.1 = (bf16[32,1536]{1,0:T(8,128)(2,1)S(1)}, bf16[2048,128]{1,0:T(8,128)(2,1)S(1)}, bf16[2048,128]{1,0:T(8,128)(2,1)S(1)}, bf16[2048,128]{1,0:T(8,128)(2,1)S(1)}, bf16[2048,128]{1,0:T(8,128)(2,1)S(1)}) custom-call(s32[32]{0:T(128)} %len_h.1, bf16[32,1536]{1,0:T(8,128)(2,1)} %hid_h.1, s32[2,8,32]{2,1,0:T(8,128)} %bitcast.47, ...), custom_call_target="tpu_custom_call" | custom-call | tf_op jit(solution)/shard_map/decode_step/pallas_call | solution.py:522
  55.5 1.4 %finish.1 = (bf16[32,1536]{1,0:T(8,128)(2,1)}, bf16[2048,128]{1,0:T(8,128)(2,1)}, bf16[2048,128]{1,0:T(8,128)(2,1)}, bf16[2048,128]{1,0:T(8,128)(2,1)}, bf16[2048,128]{1,0:T(8,128)(2,1)}) custom-call(bf16[32,1536]{1,0:T(8,128)(2,1)S(1)} %get-tuple-element.15.refs_0_, bf16[2048,128]{1,0:T(8,128)(2,1)S(1)} %get-tuple-element.16.refs_1_, ...), custom_call_target="tpu_custom_call" | custom-call | tf_op jit(solution)/shard_map/finish/pallas_call | solution.py:532
